TPU v7x, 32 devices: a whole 2x2x4 slice. The times are simulated.
32 devices in a mesh: dp: 8 (over y, x, core), tensor: 4 (over z).
Axes of the slice: x: 2, y: 2, z: 4, core: 2. Of those that a mesh axis runs over, the one named last changes fastest.
Arguments:
- block_input: bfloat16 [4096, 2048], P(('dp', 'tensor')), may hold values from -6 to 6
- norm1_gain: float32 [2048], replicated, may hold values from 0.5 to 1.5
- norm1_bias: float32 [2048], replicated, may hold values from -2 to 2
- qkv_weight: bfloat16 [2048, 3, 2048], P(None, None, 'tensor'), may hold values from -0.125 to 0.125
- qkv_bias: float32 [3, 2048], P(None, 'tensor'), may hold values from -2 to 2
- out_weight: bfloat16 [2048, 2048], P('tensor'), may hold values from -0.375 to 0.375
- norm2_gain: float32 [2048], replicated, may hold values from 0.5 to 1.5
- norm2_bias: float32 [2048], replicated, may hold values from -2 to 2
- gate_weight: bfloat16 [2048, 5632], P(None, 'tensor'), may hold values from -0.125 to 0.125
- up_weight: bfloat16 [2048, 5632], P(None, 'tensor'), may hold values from -0.125 to 0.125
- down_weight: bfloat16 [5632, 2048], P('tensor'), may hold values from -0.078125 to 0.078125
- cotangent: bfloat16 [4096, 2048], P(('dp', 'tensor')), may hold values from -6 to 6
Outputs:
- block_output: bfloat16 [4096, 2048], P(('dp', 'tensor'))
- input_grad: float32 [4096, 2048], P(('dp', 'tensor'))
- norm1_gain_grad: float32 [2048], replicated
- norm1_bias_grad: float32 [2048], replicated
- qkv_weight_grad: float32 [2048, 3, 2048], P(None, None, 'tensor')
- qkv_bias_grad: float32 [3, 2048], P(None, 'tensor')
- out_weight_grad: float32 [2048, 2048], P('tensor')
- norm2_gain_grad: float32 [2048], replicated
- norm2_bias_grad: float32 [2048], replicated
- gate_weight_grad: float32 [2048, 5632], P(None, 'tensor')
- up_weight_grad: float32 [2048, 5632], P(None, 'tensor')
- down_weight_grad: float32 [5632, 2048], P('tensor')
All inputs are finite; a program needn't handle non-finite values.
Results may differ from a plain program's by a relative error of at most 0.014.
Values may be sent and summed in bfloat16 or wider, within the bound.
A program may use at most 320 MiB of HBM per device.

v0:
```python
import jax
import jax.numpy as jnp
from jax import lax
from jax.sharding import PartitionSpec as P

HD = 64
ROT = 16
LEN = 512


epsilon = 1e-05
rotary_base = 10000.0


def layer_norm(stream, norm_gain, norm_shift):
    center = jnp.mean(stream, axis=-1, keepdims=True)
    offset = stream - center
    inverse = lax.rsqrt(jnp.mean(offset * offset, axis=-1, keepdims=True) + epsilon)
    scaled = offset * inverse
    return (scaled * norm_gain + norm_shift, scaled, inverse)


def norm_back(grad_out, scaled, inverse, norm_gain):
    weighted = grad_out * norm_gain
    centred = weighted - jnp.mean(weighted, axis=-1, keepdims=True)
    return inverse * (centred - scaled * jnp.mean(weighted * scaled, axis=-1, keepdims=True))


def rotary_tables(length, rotated):
    half_width = rotated // 2
    frequency = rotary_base ** (-(jnp.arange(half_width, dtype=jnp.float32) * 2.0 / rotated))
    angles = jnp.arange(length, dtype=jnp.float32)[:, None] * frequency[None, :]
    cosine = jnp.concatenate([jnp.cos(angles), jnp.cos(angles)], axis=-1)
    sine_table = jnp.concatenate([jnp.sin(angles), jnp.sin(angles)], axis=-1)
    return (cosine[:, None, :], sine_table[:, None, :])


def rotate(vector, cosine, sine_table):
    rotated = cosine.shape[-1]
    half_width = rotated // 2
    leading = vector[..., :rotated]
    turned = jnp.concatenate([-leading[..., half_width:], leading[..., :half_width]], axis=-1)
    return jnp.concatenate([leading * cosine + turned * sine_table, vector[..., rotated:]], axis=-1)


def rotate_back(grad_vec, cosine, sine_table):
    rotated = cosine.shape[-1]
    half_width = rotated // 2
    leading = grad_vec[..., :rotated]
    moved = leading * sine_table
    turned = jnp.concatenate([moved[..., half_width:], -moved[..., :half_width]], axis=-1)
    return jnp.concatenate([leading * cosine + turned, grad_vec[..., rotated:]], axis=-1)


def product(left, right, left_dim, right_dim):
    return lax.dot_general(
        left, right, (((left_dim,), (right_dim,)), ((), ())), preferred_element_type=jnp.float32
    )


def masked_scores(query, keys, scale):
    length = query.shape[1]
    scores = jnp.einsum("sqhd,skhd->shqk", query, keys, preferred_element_type=jnp.float32) * scale
    causal = lax.broadcasted_iota(jnp.int32, (length, length), 0) >= lax.broadcasted_iota(
        jnp.int32, (length, length), 1
    )
    return jnp.where(causal, scores, -1e30)


def body(
    block_input,
    norm1_gain,
    norm1_bias,
    qkv_weight,
    qkv_bias,
    out_weight,
    norm2_gain,
    norm2_bias,
    gate_weight,
    up_weight,
    down_weight,
    cotangent,
):
    width = block_input.shape[1]
    inner = qkv_weight.shape[2]
    local_heads = inner // HD
    scale = HD ** (-0.5)
    flat_qkv = qkv_weight.reshape(width, 3 * inner)
    cosine, sine_table = rotary_tables(LEN, ROT)
    stream = block_input.astype(jnp.float32)
    normed, scaled_one, inverse_one = layer_norm(stream, norm1_gain, norm1_bias)
    normed_one = normed.astype(jnp.bfloat16)
    rows_one = lax.all_gather(normed_one, "tensor", axis=0, tiled=True)
    group = rows_one.shape[0]
    seq_count = group // LEN
    projected = jnp.dot(rows_one, flat_qkv, preferred_element_type=jnp.float32) + qkv_bias.reshape(
        3 * inner
    )
    projected = projected.reshape(seq_count, LEN, 3, local_heads, HD)
    query = rotate(projected[:, :, 0], cosine, sine_table).astype(jnp.bfloat16)
    keys = rotate(projected[:, :, 1], cosine, sine_table).astype(jnp.bfloat16)
    values = projected[:, :, 2].astype(jnp.bfloat16)
    scores = masked_scores(query, keys, scale)
    highest = jnp.max(scores, axis=-1, keepdims=True)
    logsum = highest + jnp.log(jnp.sum(jnp.exp(scores - highest), axis=-1, keepdims=True))
    weights = jnp.exp(scores - logsum).astype(jnp.bfloat16)
    mixed_heads = jnp.einsum(
        "shqk,skhd->sqhd", weights, values, preferred_element_type=jnp.float32
    ).astype(jnp.bfloat16)
    mixed = mixed_heads.reshape(group, inner)
    attended = stream + lax.psum_scatter(
        jnp.dot(mixed, out_weight, preferred_element_type=jnp.float32),
        "tensor",
        scatter_dimension=0,
        tiled=True,
    )
    normed, scaled_two, inverse_two = layer_norm(attended, norm2_gain, norm2_bias)
    normed_two = normed.astype(jnp.bfloat16)
    rows_two = lax.all_gather(normed_two, "tensor", axis=0, tiled=True)
    gate = jnp.dot(rows_two, gate_weight, preferred_element_type=jnp.float32)
    upward = jnp.dot(rows_two, up_weight, preferred_element_type=jnp.float32)
    hidden = (jax.nn.silu(gate) * upward).astype(jnp.bfloat16)
    block_output = (
        attended
        + lax.psum_scatter(
            jnp.dot(hidden, down_weight, preferred_element_type=jnp.float32).astype(jnp.bfloat16),
            "tensor",
            scatter_dimension=0,
            tiled=True,
        ).astype(jnp.float32)
    ).astype(jnp.bfloat16)
    grad_rows = lax.all_gather(cotangent, "tensor", axis=0, tiled=True)
    grad_hidden = product(grad_rows, down_weight, 1, 1)
    gate_sigmoid = jax.nn.sigmoid(gate)
    grad_gate = (grad_hidden * upward * gate_sigmoid * (1.0 + gate * (1.0 - gate_sigmoid))).astype(
        jnp.bfloat16
    )
    grad_up = (grad_hidden * gate * gate_sigmoid).astype(jnp.bfloat16)
    down_grad = product(hidden, grad_rows, 0, 0)
    gate_grad = product(rows_two, grad_gate, 0, 0)
    up_grad = product(rows_two, grad_up, 0, 0)
    grad_normed_two = lax.psum_scatter(
        product(grad_gate, gate_weight, 1, 1) + product(grad_up, up_weight, 1, 1),
        "tensor",
        scatter_dimension=0,
        tiled=True,
    )
    norm2_gain_part = jnp.sum(grad_normed_two * scaled_two, axis=0)
    norm2_bias_part = jnp.sum(grad_normed_two, axis=0)
    grad_stream = cotangent.astype(jnp.float32) + norm_back(
        grad_normed_two, scaled_two, inverse_two, norm2_gain
    )
    grad_low = grad_stream.astype(jnp.bfloat16)
    grad_attended = lax.all_gather(grad_low, "tensor", axis=0, tiled=True)
    out_grad = product(mixed, grad_attended, 0, 0)
    grad_mixed = (
        product(grad_attended, out_weight, 1, 1)
        .astype(jnp.bfloat16)
        .reshape(seq_count, LEN, local_heads, HD)
    )
    scores = masked_scores(query, keys, scale)
    probs = jnp.exp(scores - logsum)
    weights = probs.astype(jnp.bfloat16)
    delta = jnp.einsum(
        "sqhd,sqhd->shq", grad_mixed, mixed_heads, preferred_element_type=jnp.float32
    )[..., None]
    grad_weights = jnp.einsum(
        "sqhd,skhd->shqk", grad_mixed, values, preferred_element_type=jnp.float32
    )
    grad_scores = (probs * (grad_weights - delta) * scale).astype(jnp.bfloat16)
    grad_query = jnp.einsum(
        "shqk,skhd->sqhd", grad_scores, keys, preferred_element_type=jnp.float32
    )
    grad_keys = jnp.einsum(
        "shqk,sqhd->skhd", grad_scores, query, preferred_element_type=jnp.float32
    )
    grad_values = jnp.einsum(
        "shqk,sqhd->skhd", weights, grad_mixed, preferred_element_type=jnp.float32
    )
    grad_projected = jnp.stack(
        [
            rotate_back(grad_query, cosine, sine_table),
            rotate_back(grad_keys, cosine, sine_table),
            grad_values,
        ],
        axis=2,
    )
    bias_grad = jnp.sum(grad_projected, axis=(0, 1)).reshape(3, inner)
    grad_flat = grad_projected.reshape(group, 3 * inner).astype(jnp.bfloat16)
    qkv_grad = product(rows_one, grad_flat, 0, 0).reshape(width, 3, inner)
    grad_normed_one = lax.psum_scatter(
        product(grad_flat, flat_qkv, 1, 1), "tensor", scatter_dimension=0, tiled=True
    )
    norm1_gain_part = jnp.sum(grad_normed_one * scaled_one, axis=0)
    norm1_bias_part = jnp.sum(grad_normed_one, axis=0)
    input_grad = grad_stream + norm_back(grad_normed_one, scaled_one, inverse_one, norm1_gain)
    norm1_gain_grad, norm1_bias_grad, norm2_gain_grad, norm2_bias_grad = lax.psum(
        (norm1_gain_part, norm1_bias_part, norm2_gain_part, norm2_bias_part), ("dp", "tensor")
    )
    qkv_grad, bias_grad, out_grad, gate_grad, up_grad, down_grad = lax.psum(
        (qkv_grad, bias_grad, out_grad, gate_grad, up_grad, down_grad), "dp"
    )
    return (
        block_output,
        input_grad,
        norm1_gain_grad,
        norm1_bias_grad,
        qkv_grad,
        bias_grad,
        out_grad,
        norm2_gain_grad,
        norm2_bias_grad,
        gate_grad,
        up_grad,
        down_grad,
    )


def solution(mesh):
    in_specs = (
        P(("dp", "tensor"), None),
        P(),
        P(),
        P(None, None, "tensor"),
        P(None, "tensor"),
        P("tensor", None),
        P(),
        P(),
        P(None, "tensor"),
        P(None, "tensor"),
        P("tensor", None),
        P(("dp", "tensor"), None),
    )
    out_specs = (
        P(("dp", "tensor"), None),
        P(("dp", "tensor"), None),
        P(),
        P(),
        P(None, None, "tensor"),
        P(None, "tensor"),
        P("tensor", None),
        P(),
        P(),
        P(None, "tensor"),
        P(None, "tensor"),
        P("tensor", None),
    )
    return jax.shard_map(body, mesh=mesh, in_specs=in_specs, out_specs=out_specs, check_vma=False)
```

profile of v0, /device:TPU:0, one launch (start us, length us, event | category | flops | bytes accessed | tf_op | source)
XLA Modules:
  0.0 1201.1 jit_solution(17748133852242335363)
XLA Ops:
  10.5 2.3 fusion.13
  13.5 8.8 copy.33
  23.1 38.1 %all-gather.5.cloned.1.call-done = bf16[512,2048]{1,0:T(8,128)(2,1)} async-done(((bf16[128,2048]{1,0:T(8,128)(2,1)}), bf16[512,2048]{1,0:T(8,128)(2,1)}) %all-gather.5.cloned.1.call-update) | async-done | bytes 2097168 | tf_op jit(solution)/shard_map/all_gather | solution.py:93
  61.3 8.5 convolution_add_fusion
  69.8 3.5 copy.34
  73.4 1.8 slice_bitcast_fusion.1
  75.5 1.5 fusion.1
  77.0 1.7 exponential_reduce_fusion
  78.8 1.6 copy-done.3
  80.4 3.5 convolution_convert_fusion.2
  84.8 3.3 fusion.44
  88.6 75.2 %reduce-scatter.5.cloned.1.call-done = f32[128,2048]{1,0:T(8,128)} async-done(((f32[512,2048]{1,0:T(8,128)}), f32[128,2048]{1,0:T(8,128)}) %reduce-scatter.5.cloned.1.call-update) | async-done | bytes 1048592 | tf_op jit(solution)/shard_map/reduce_scatter | solution.py:111
  163.9 1.5 fusion.41
  168.1 45.7 %all-gather.7.cloned.1.call-done = bf16[512,2048]{1,0:T(8,128)(2,1)} async-done(((bf16[128,2048]{1,0:T(8,128)(2,1)}), bf16[512,2048]{1,0:T(8,128)(2,1)}) %all-gather.7.cloned.1.call-update) | async-done | bytes 2097168 | tf_op jit(solution)/shard_map/all_gather | solution.py:119
  213.8 8.4 fusion.46
  222.2 7.7 fusion.45
  229.9 29.8 %all-gather.9.cloned.1.call-done = bf16[512,2048]{1,0:T(8,128)(2,1)} async-done(((bf16[128,2048]{1,0:T(8,128)(2,1)}), bf16[512,2048]{1,0:T(8,128)(2,1)}) %all-gather.9.cloned.1.call-update) | async-done | bytes 2097168 | tf_op jit(solution)/shard_map/all_gather | solution.py:132
  259.7 10.4 multiply_convert_fusion.1
  270.1 6.5 fusion.47
  276.7 7.7 convolution_add_fusion.1
  284.7 7.8 convolution_convert_fusion
  292.6 67.6 %reduce-scatter.9.cloned.1.call-done = f32[128,2048]{1,0:T(8,128)} async-done(((f32[512,2048]{1,0:T(8,128)}), f32[128,2048]{1,0:T(8,128)}) %reduce-scatter.9.cloned.1.call-update) | async-done | bytes 1048592 | tf_op jit(solution)/shard_map/reduce_scatter | solution.py:142
  360.2 2.3 multiply_reduce_fusion
  363.5 43.6 %reduce-scatter.7.cloned.1.call-done = bf16[128,2048]{1,0:T(8,128)(2,1)} async-done(((bf16[512,2048]{1,0:T(8,128)(2,1)}), bf16[128,2048]{1,0:T(8,128)(2,1)}) %reduce-scatter.7.cloned.1.call-update) | async-done | bytes 524304 | tf_op jit(solution)/shard_map/reduce_scatter | solution.py:125
  407.1 3.5 fusion.40
  410.7 44.9 %all-gather.11.cloned.1.call-done = bf16[512,2048]{1,0:T(8,128)(2,1)} async-done(((bf16[128,2048]{1,0:T(8,128)(2,1)}), bf16[512,2048]{1,0:T(8,128)(2,1)}) %all-gather.11.cloned.1.call-update) | async-done | bytes 2097168 | tf_op jit(solution)/shard_map/all_gather | solution.py:154
  455.6 3.1 fusion.20
  458.8 5.7 convolution_bitcast_fusion
  464.5 4.9 multiply_convert_fusion
  469.5 1.4 convolution_bitcast_fusion.1
  475.4 5.0 fusion.48
  480.7 9.8 fusion.52
  490.5 6.3 fusion.51
  496.8 6.3 fusion.50
  503.1 3.2 fusion.49
  506.3 6.6 fusion.4
  513.0 1.6 fusion.2
  514.6 15.1 %psum.73 = f32[3,512]{1,0:T(4,128)} all-reduce(f32[3,512]{1,0:T(4,128)S(1)} %reshape.309), channel_id=1, replica_groups=mesh['dp'=8,'tensor'=4] {'dp'}, use_global_device_ids=true, to_apply=%region_20.21 | all-reduce | flops 1536 | bytes 12288 | tf_op jit(solution)/shard_map/psum | solution.py:200
  529.7 26.4 %reduce-scatter.11.cloned.1.call-done = f32[128,2048]{1,0:T(8,128)} async-done(((f32[512,2048]{1,0:T(8,128)}), f32[128,2048]{1,0:T(8,128)}) %reduce-scatter.11.cloned.1.call-update) | async-done | bytes 1048592 | tf_op jit(solution)/shard_map/reduce_scatter | solution.py:191
  556.2 1.7 fusion.18
  557.9 42.8 %all-reduce = (f32[2048]{0:T(1024)}, f32[2048]{0:T(1024)}, f32[2048]{0:T(1024)}, f32[2048]{0:T(1024)}) all-reduce(f32[2048]{0:T(1024)S(1)} %get-tuple-element.14, f32[2048]{0:T(1024)S(1)} %get-tuple-element.19, f32[2048]{0:T(1024)S(1)} %get-tuple-element.12, f32[2048]{0:T(1024)S(1)} %copy-done.25), channel_id=1, replica_groups=mesh['dp'=8,'tensor'=4] {'dp','tensor'}, use_global_device_ids=true, to_apply=%region_15.16 | all-reduce | flops 8192 | bytes 65536 | tf_op jit(solution)/shard_map/psum | solution.py:197
  600.7 3.0 fusion.17
  603.6 547.8 %all-reduce.4.cloned.1.call-done = (f32[2048,3,512]{2,0,1:T(8,128)}, f32[512,2048]{1,0:T(8,128)}, f32[2048,1408]{1,0:T(8,128)}, f32[2048,1408]{1,0:T(8,128)}, f32[1408,2048]{1,0:T(8,128)}) async-done(((f32[2048,3,512]{2,0,1:T(8,128)}, f32[512,2048]{1,0:T(8,128)}, f32[2048,1408]{1,0:T(8,128)}, f32[2048,1408]{1,0:T(8,128)}, f32[1408,2048]{1,0:T(8,128)}), (f32[2048,3,512]{2,0,1:T(8,128)}, ...) | async-done | bytes 51380240 | tf_op jit(solution)/shard_map/psum | solution.py:200
  1151.4 11.1 copy.60
  1162.4 2.0 copy.61
  1164.5 9.4 copy.62
  1173.9 9.4 copy.63
  1183.4 10.8 copy.64
  (143 shorter events, 15.5 us)
Async XLA Ops:
  7.2 77.6 %copy-start = (bf16[512,2048]{1,0:T(8,128)(2,1)S(1)}, bf16[512,2048]{1,0:T(8,128)(2,1)}, u32[]{:S(2)}) copy-start(bf16[512,2048]{1,0:T(8,128)(2,1)} %param.17) | copy-start | bytes 6291460
  7.2 54.1 %all-gather.5.cloned.1.call-start = ((), (), s32[]{:S(2)}) async-start(), calls=%async_computation.4 | async-start | bytes 2621440 | tf_op jit(solution)/shard_map/all_gather | solution.py:93
  8.6 1.3 copy-start.29
  12.8 151.1 %reduce-scatter.5.cloned.1.call-start = ((), (), s32[]{:S(2)}) async-start(), calls=%async_computation.5 | async-start | bytes 5242880 | tf_op jit(solution)/shard_map/reduce_scatter | solution.py:111
  23.1 55.6 %copy-start.13 = (pred[512,512]{0,1:T(8,128)(4,1)}, pred[512,512]{0,1:T(8,128)(4,1)S(1)}, u32[]{:S(2)}) copy-start(pred[512,512]{0,1:T(8,128)(4,1)S(1)} %iota_compare_fusion) | copy-start | bytes 786436
  73.4 1.9 copy-start.19
  73.4 2.0 copy-start.21
  75.3 1.7 copy-start.9
  75.5 1.5 copy-start.15
  75.5 1.5 copy-start.17
  77.0 3.4 copy-start.3
  80.4 3.5 copy-start.26
  88.1 78.4 %copy-start.23 = (f32[2048]{0:T(1024)S(1)}, f32[2048]{0:T(1024)}, u32[]{:S(2)}) copy-start(f32[2048]{0:T(1024)} %param.18) | copy-start | bytes 24580
  88.1 78.4 %copy-start.31 = (f32[2048]{0:T(1024)S(1)}, f32[2048]{0:T(1024)}, u32[]{:S(2)}) copy-start(f32[2048]{0:T(1024)} %param.19) | copy-start | bytes 24580
  88.1 125.7 %all-gather.7.cloned.1.call-start = ((), (), s32[]{:S(2)}) async-start(), calls=%async_computation.6 | async-start | bytes 2621440 | tf_op jit(solution)/shard_map/all_gather | solution.py:119
  167.5 92.2 %all-gather.9.cloned.1.call-start = ((), (), s32[]{:S(2)}) async-start(), calls=%async_computation.8 | async-start | bytes 2621440 | tf_op jit(solution)/shard_map/all_gather | solution.py:132
  168.1 192.1 %reduce-scatter.9.cloned.1.call-start = ((), (), s32[]{:S(2)}) async-start(), calls=%async_computation.9 | async-start | bytes 5242880 | tf_op jit(solution)/shard_map/reduce_scatter | solution.py:142
  213.8 8.4 copy-start.36
  270.1 6.5 copy-start.38
  270.1 6.6 copy-start.40
  284.4 122.6 %reduce-scatter.7.cloned.1.call-start = ((), (), s32[]{:S(2)}) async-start(), calls=%async_computation.7 | async-start | bytes 2621440 | tf_op jit(solution)/shard_map/reduce_scatter | solution.py:125
  292.5 163.1 %all-gather.11.cloned.1.call-start = ((), (), s32[]{:S(2)}) async-start(), calls=%async_computation.10 | async-start | bytes 2621440 | tf_op jit(solution)/shard_map/all_gather | solution.py:154
  410.6 48.1 %copy-start.14 = (pred[512,512]{0,1:T(8,128)(4,1)S(1)}, pred[512,512]{0,1:T(8,128)(4,1)}, u32[]{:S(2)}) copy-start(pred[512,512]{0,1:T(8,128)(4,1)} %copy-done.13) | copy-start | bytes 786436
  410.6 48.1 %copy-start.27 = (f32[8,512]{1,0:T(8,128)S(1)}, f32[8,512]{1,0:T(8,128)}, u32[]{:S(2)}) copy-start(f32[8,512]{1,0:T(8,128)} %copy-done.26) | copy-start | bytes 49156
  410.7 145.5 %reduce-scatter.11.cloned.1.call-start = ((), (), s32[]{:S(2)}) async-start(), calls=%async_computation.11 | async-start | bytes 5242880 | tf_op jit(solution)/shard_map/reduce_scatter | solution.py:191
  455.6 8.8 slice-start
  458.8 5.7 slice-start.1
  464.5 8.3 copy-start.5
  464.5 4.9 copy-start.10
  464.5 4.9 copy-start.18
  469.4 1.4 copy-start.16
  471.8 2.5 slice-start.2
  472.6 2.8 slice-start.3
  480.4 671.0 %all-reduce.4.cloned.1.call-start = ((), (), s32[]{:S(2)}) async-start(), calls=%async_computation.12 | async-start | bytes 102760448 | tf_op jit(solution)/shard_map/psum | solution.py:200
  480.7 9.8 copy-start.37
  480.7 9.8 copy-start.41
  490.5 6.3 copy-start.39
  496.8 6.3 copy-start.6
  496.8 6.3 copy-start.8
  503.1 3.2 copy-start.12
  503.1 3.2 copy-start.35
  512.9 43.2 %copy-start.2 = (bf16[128,2048]{1,0:T(8,128)(2,1)S(1)}, bf16[128,2048]{1,0:T(8,128)(2,1)}, u32[]{:S(2)}) copy-start(bf16[128,2048]{1,0:T(8,128)(2,1)} %param.12) | copy-start | bytes 1572868
  513.0 43.2 %copy-start.24 = (f32[2048]{0:T(1024)S(1)}, f32[2048]{0:T(1024)}, u32[]{:S(2)}) copy-start(f32[2048]{0:T(1024)} %param.13) | copy-start | bytes 24580
  513.0 43.2 %copy-start.30 = (f32[128]{0:T(128)S(1)}, f32[128]{0:T(128)}, u32[]{:S(2)}) copy-start(f32[128]{0:T(128)} %copy-done.29) | copy-start | bytes 1540
  513.0 43.2 %copy-start.33 = (f32[128]{0:T(128)S(1)}, f32[128]{0:T(128)}, u32[]{:S(2)}) copy-start(f32[128]{0:T(128)} %copy-done.32) | copy-start | bytes 1540
  513.0 44.9 %copy-start.25 = (f32[2048]{0:T(1024)S(1)}, f32[2048]{0:T(1024)}, u32[]{:S(2)}) copy-start(f32[2048]{0:T(1024)} %get-tuple-element.18) | copy-start | bytes 24580
  1151.4 11.1 copy-start.4
  1183.4 10.8 copy-start.1
  (7 other events, 5.2 us)
Sparse Core Ops, SparseCore 0:
  12.9 48.3 all-gather.4
  88.2 75.5 reduce-scatter.4
  167.6 46.1 all-gather.6
  215.2 44.4 all-gather.8
  284.6 75.5 reduce-scatter.8
  362.9 44.1 reduce-scatter.6
  410.8 44.8 all-gather.10
  480.5 75.5 reduce-scatter.10
  562.0 589.3 all-reduce.3
where the time goes:
time: 1210 us; the launch traced here: 1200 us
  waiting for transfers between devices  920 us (76%)
  matrix products  119 us (10%)
  local copies, waits for them, and re-layouts  64.4 us (5%)
  blocking collectives  57.9 us (5%)
  other arithmetic  24.3 us (2%)
  between operations  14.9 us (1%)
    psum x1, waiting for transfers between devices, body(): lax.psum((qkv_grad, bias_grad, out_grad, gate_grad, up_grad, down_grad),...  548 us
    reduce_scatter x1, waiting for transfers between devices, body(): lax.psum_scatter(jnp.dot(mixed, out_weight, preferred_element_type=jnp.fl...  75.2 us
    reduce_scatter x1, waiting for transfers between devices, body(): lax.psum_scatter(product(grad_gate, gate_weight, 1, 1) + product(grad_up,...  67.6 us
    dot_general x10, matrix products, product(): lax.dot_general(left, right, (((left_dim,), (right_dim,)), ((), ())), pre...  64.9 us
    unnamed x98, local copies, waits for them, and re-layouts  58.1 us
    all_gather x1, waiting for transfers between devices, body(): rows_two = lax.all_gather(normed_two, 'tensor', axis=0, tiled=True)  45.7 us
    all_gather x1, waiting for transfers between devices, body(): grad_attended = lax.all_gather(grad_low, 'tensor', axis=0, tiled=True)  44.9 us
    reduce_scatter x1, waiting for transfers between devices, body(): lax.psum_scatter(jnp.dot(hidden, down_weight, preferred_element_type=jnp....  43.6 us
  transfers between devices with their start and end apart: 9, of which 9 were waited for; matrix products, arithmetic and copies ran while one was open for 6% of the time, Pallas kernels for 0%

commit v1 on v0

--- a/solution.py
+++ b/solution.py
@@ -1,3 +1,5 @@
+import functools
+
 import jax
 import jax.numpy as jnp
 from jax import lax
@@ -67,7 +69,68 @@
     return jnp.where(causal, scores, -1e30)
 
 
+def halving_masks(ways):
+    masks = [1 << bit for bit in range(ways.bit_length() - 1)]
+    return masks[:1] + masks[1:], masks[:1] + masks[1:][::-1]
+
+
+class Halver:
+    def __init__(self, axis, ways):
+        self.axis, self.ways = axis, ways
+        self.even, self.odd = halving_masks(ways)
+        index = lax.axis_index(axis)
+        odd = index % 2 == 1
+        self.keeps = []
+        for even_mask, odd_mask in zip(self.even, self.odd):
+            mask = jnp.where(odd, odd_mask, even_mask)
+            self.keeps.append(((index // mask) % 2).astype(jnp.int32))
+
+    def swap(self, value, level):
+        pairs = [
+            (i, i ^ (self.odd[level] if i % 2 else self.even[level])) for i in range(self.ways)
+        ]
+        return lax.ppermute(value, self.axis, pairs)
+
+    def reduce(self, left, right):
+        rows = left.shape[1]
+        held, offset, arrived = rows, jnp.int32(0), []
+        for level, keep in enumerate(self.keeps):
+            half = held // 2
+            away = offset + (1 - keep) * half
+            offset = offset + keep * half
+            total = self.block(left, right, away, half, arrived)
+            arrived = [(got, base, size) for got, base, size in arrived]
+            got = self.swap(total.astype(jnp.bfloat16), level)
+            arrived.append((got, offset, half))
+            held = half
+        return self.block(left, right, offset, held, arrived).astype(jnp.bfloat16)
+
+    def block(self, left, right, start, size, arrived):
+        total = product(lax.dynamic_slice_in_dim(left, start, size, 1), right, 0, 0)
+        for got, base, _ in arrived:
+            total = total + lax.dynamic_slice_in_dim(got, start - base, size, 0).astype(jnp.float32)
+        return total
+
+    def spread(self, piece):
+        for level in range(len(self.keeps) - 1, -1, -1):
+            keep = self.keeps[level]
+            other = self.swap(piece, level)
+            size = piece.shape[0]
+            kind = jnp.float32 if level == 0 else jnp.bfloat16
+            whole = jnp.zeros((2 * size,) + piece.shape[1:], kind)
+            whole = lax.dynamic_update_slice_in_dim(whole, piece.astype(kind), keep * size, 0)
+            piece = lax.dynamic_update_slice_in_dim(whole, other.astype(kind), (1 - keep) * size, 0)
+        return piece
+
+
+def scatter_sum(value):
+    return lax.psum_scatter(
+        value.astype(jnp.bfloat16), "tensor", scatter_dimension=0, tiled=True
+    ).astype(jnp.float32)
+
+
 def body(
+    ways,
     block_input,
     norm1_gain,
     norm1_bias,
@@ -85,7 +148,8 @@
     inner = qkv_weight.shape[2]
     local_heads = inner // HD
     scale = HD ** (-0.5)
-    flat_qkv = qkv_weight.reshape(width, 3 * inner)
+    parts = [qkv_weight[:, i] for i in range(3)]
+    halver = Halver("dp", ways)
     cosine, sine_table = rotary_tables(LEN, ROT)
     stream = block_input.astype(jnp.float32)
     normed, scaled_one, inverse_one = layer_norm(stream, norm1_gain, norm1_bias)
@@ -93,13 +157,15 @@
     rows_one = lax.all_gather(normed_one, "tensor", axis=0, tiled=True)
     group = rows_one.shape[0]
     seq_count = group // LEN
-    projected = jnp.dot(rows_one, flat_qkv, preferred_element_type=jnp.float32) + qkv_bias.reshape(
-        3 * inner
-    )
-    projected = projected.reshape(seq_count, LEN, 3, local_heads, HD)
-    query = rotate(projected[:, :, 0], cosine, sine_table).astype(jnp.bfloat16)
-    keys = rotate(projected[:, :, 1], cosine, sine_table).astype(jnp.bfloat16)
-    values = projected[:, :, 2].astype(jnp.bfloat16)
+    projected = [
+        (jnp.dot(rows_one, part, preferred_element_type=jnp.float32) + bias).reshape(
+            seq_count, LEN, local_heads, HD
+        )
+        for part, bias in zip(parts, qkv_bias)
+    ]
+    query = rotate(projected[0], cosine, sine_table).astype(jnp.bfloat16)
+    keys = rotate(projected[1], cosine, sine_table).astype(jnp.bfloat16)
+    values = projected[2].astype(jnp.bfloat16)
     scores = masked_scores(query, keys, scale)
     highest = jnp.max(scores, axis=-1, keepdims=True)
     logsum = highest + jnp.log(jnp.sum(jnp.exp(scores - highest), axis=-1, keepdims=True))
@@ -108,12 +174,7 @@
         "shqk,skhd->sqhd", weights, values, preferred_element_type=jnp.float32
     ).astype(jnp.bfloat16)
     mixed = mixed_heads.reshape(group, inner)
-    attended = stream + lax.psum_scatter(
-        jnp.dot(mixed, out_weight, preferred_element_type=jnp.float32),
-        "tensor",
-        scatter_dimension=0,
-        tiled=True,
-    )
+    attended = stream + scatter_sum(jnp.dot(mixed, out_weight, preferred_element_type=jnp.float32))
     normed, scaled_two, inverse_two = layer_norm(attended, norm2_gain, norm2_bias)
     normed_two = normed.astype(jnp.bfloat16)
     rows_two = lax.all_gather(normed_two, "tensor", axis=0, tiled=True)
@@ -121,13 +182,7 @@
     upward = jnp.dot(rows_two, up_weight, preferred_element_type=jnp.float32)
     hidden = (jax.nn.silu(gate) * upward).astype(jnp.bfloat16)
     block_output = (
-        attended
-        + lax.psum_scatter(
-            jnp.dot(hidden, down_weight, preferred_element_type=jnp.float32).astype(jnp.bfloat16),
-            "tensor",
-            scatter_dimension=0,
-            tiled=True,
-        ).astype(jnp.float32)
+        attended + scatter_sum(jnp.dot(hidden, down_weight, preferred_element_type=jnp.float32))
     ).astype(jnp.bfloat16)
     grad_rows = lax.all_gather(cotangent, "tensor", axis=0, tiled=True)
     grad_hidden = product(grad_rows, down_weight, 1, 1)
@@ -136,15 +191,12 @@
         jnp.bfloat16
     )
     grad_up = (grad_hidden * gate * gate_sigmoid).astype(jnp.bfloat16)
-    down_grad = product(hidden, grad_rows, 0, 0)
-    gate_grad = product(rows_two, grad_gate, 0, 0)
-    up_grad = product(rows_two, grad_up, 0, 0)
-    grad_normed_two = lax.psum_scatter(
-        product(grad_gate, gate_weight, 1, 1) + product(grad_up, up_weight, 1, 1),
-        "tensor",
-        scatter_dimension=0,
-        tiled=True,
-    )
+    grad_normed_two = scatter_sum(
+        product(grad_gate, gate_weight, 1, 1) + product(grad_up, up_weight, 1, 1)
+    )
+    down_piece = halver.reduce(hidden, grad_rows)
+    gate_piece = halver.reduce(rows_two, grad_gate)
+    up_piece = halver.reduce(rows_two, grad_up)
     norm2_gain_part = jnp.sum(grad_normed_two * scaled_two, axis=0)
     norm2_bias_part = jnp.sum(grad_normed_two, axis=0)
     grad_stream = cotangent.astype(jnp.float32) + norm_back(
@@ -152,7 +204,7 @@
     )
     grad_low = grad_stream.astype(jnp.bfloat16)
     grad_attended = lax.all_gather(grad_low, "tensor", axis=0, tiled=True)
-    out_grad = product(mixed, grad_attended, 0, 0)
+    out_piece = halver.reduce(mixed, grad_attended)
     grad_mixed = (
         product(grad_attended, out_weight, 1, 1)
         .astype(jnp.bfloat16)
@@ -177,29 +229,31 @@
     grad_values = jnp.einsum(
         "shqk,sqhd->skhd", weights, grad_mixed, preferred_element_type=jnp.float32
     )
-    grad_projected = jnp.stack(
-        [
+    grad_projected = [
+        piece.reshape(group, inner)
+        for piece in (
             rotate_back(grad_query, cosine, sine_table),
             rotate_back(grad_keys, cosine, sine_table),
             grad_values,
-        ],
-        axis=2,
-    )
-    bias_grad = jnp.sum(grad_projected, axis=(0, 1)).reshape(3, inner)
-    grad_flat = grad_projected.reshape(group, 3 * inner).astype(jnp.bfloat16)
-    qkv_grad = product(rows_one, grad_flat, 0, 0).reshape(width, 3, inner)
-    grad_normed_one = lax.psum_scatter(
-        product(grad_flat, flat_qkv, 1, 1), "tensor", scatter_dimension=0, tiled=True
-    )
+        )
+    ]
+    bias_grad = jnp.stack([jnp.sum(piece, axis=0) for piece in grad_projected])
+    grad_flat = [piece.astype(jnp.bfloat16) for piece in grad_projected]
+    grad_normed_one = scatter_sum(
+        sum(product(piece, part, 1, 1) for piece, part in zip(grad_flat, parts))
+    )
+    qkv_pieces = [halver.reduce(rows_one, piece) for piece in grad_flat]
     norm1_gain_part = jnp.sum(grad_normed_one * scaled_one, axis=0)
     norm1_bias_part = jnp.sum(grad_normed_one, axis=0)
     input_grad = grad_stream + norm_back(grad_normed_one, scaled_one, inverse_one, norm1_gain)
     norm1_gain_grad, norm1_bias_grad, norm2_gain_grad, norm2_bias_grad = lax.psum(
         (norm1_gain_part, norm1_bias_part, norm2_gain_part, norm2_bias_part), ("dp", "tensor")
     )
-    qkv_grad, bias_grad, out_grad, gate_grad, up_grad, down_grad = lax.psum(
-        (qkv_grad, bias_grad, out_grad, gate_grad, up_grad, down_grad), "dp"
-    )
+    bias_grad = lax.psum(bias_grad, "dp")
+    down_grad, gate_grad, up_grad, out_grad = (
+        halver.spread(piece) for piece in (down_piece, gate_piece, up_piece, out_piece)
+    )
+    qkv_grad = jnp.stack([halver.spread(piece) for piece in qkv_pieces], axis=1)
     return (
         block_output,
         input_grad,
@@ -245,4 +299,4 @@
         P(None, "tensor"),
         P("tensor", None),
     )
-    return jax.shard_map(body, mesh=mesh, in_specs=in_specs, out_specs=out_specs, check_vma=False)
+    return jax.shard_map(functools.partial(body, mesh.shape["dp"]), mesh=mesh, in_specs=in_specs, out_specs=out_specs, check_vma=False)

time: 1210 us -> 674 us (0.56)
  waiting for transfers between devices: 920 us -> 294 us
  other arithmetic: 24.3 us -> 73.4 us
  starting transfers between devices: 1.22 us -> 34.4 us
  matrix products: 119 us -> 146 us
  local copies, waits for them, and re-layouts: 64.4 us -> 46.5 us
    psum x1 -> x0, waiting for transfers between devices: 548 us -> none  [body(): lax.psum((qkv_grad, bias_grad, out_grad, gate_grad, up_grad, down_grad),...]
    reduce_scatter x4, waiting for transfers between devices: 213 us -> 71.8 us  [scatter_sum(): lax.psum_scatter(value.astype(jnp.bfloat16), 'tensor', scatter_dimension=...]
    ppermute x0 -> x42, waiting for transfers between devices: none -> 73.1 us  [swap(): return lax.ppermute(value, self.axis, pairs)]
    unnamed x98 -> x198, local copies, waits for them, and re-layouts: 58.1 us -> 10.5 us
    dynamic_update_slice x0 -> x21, other arithmetic: none -> 45.7 us  [the longest x14 24.3 us: spread(): lax.dynamic_update_slice_in_dim(whole, piece.astype(kind), keep * size, 0)]
    ppermute x0 -> x42, starting transfers between devices: none -> 33.5 us  [swap(): return lax.ppermute(value, self.axis, pairs)]
    dot_general x10 -> x35, matrix products: 64.9 us -> 97 us  [product(): lax.dot_general(left, right, (((left_dim,), (right_dim,)), ((), ())), pre...]
    all_gather x1, waiting for transfers between devices: 44.9 us -> 26.7 us  [body(): grad_attended = lax.all_gather(grad_low, 'tensor', axis=0, tiled=True)]
  transfers between devices with their start and end apart: 9 -> 50, of which waited for: 9 -> 25; matrix products, arithmetic and copies ran while one was open for 6% -> 30% of each run, Pallas kernels for 0% -> 0%
where the time goes in v1:
time: 674 us; the launch traced here: 664 us
  waiting for transfers between devices  294 us (44%)
  matrix products  146 us (22%)
  other arithmetic  73.4 us (11%)
  blocking collectives  54.3 us (8%)
  local copies, waits for them, and re-layouts  46.5 us (7%)
  starting transfers between devices  34.4 us (5%)
  between operations  16.5 us (2%)
    dot_general x35, matrix products, product(): lax.dot_general(left, right, (((left_dim,), (right_dim,)), ((), ())), pre...  97 us
    ppermute x42, waiting for transfers between devices, swap(): return lax.ppermute(value, self.axis, pairs)  73.1 us
    reduce_scatter x4, waiting for transfers between devices, scatter_sum(): lax.psum_scatter(value.astype(jnp.bfloat16), 'tensor', scatter_dimension=...  71.8 us
    all_gather x1, waiting for transfers between devices, body(): rows_one = lax.all_gather(normed_one, 'tensor', axis=0, tiled=True)  47.5 us
    all_gather x1, waiting for transfers between devices, body(): rows_two = lax.all_gather(normed_two, 'tensor', axis=0, tiled=True)  44.4 us
    psum x1, blocking collectives, body(): lax.psum((norm1_gain_part, norm1_bias_part, norm2_gain_part, norm2_bias_p...  39.1 us
    ppermute x42, starting transfers between devices, swap(): return lax.ppermute(value, self.axis, pairs)  33.5 us
    all_gather x1, waiting for transfers between devices, body(): grad_rows = lax.all_gather(cotangent, 'tensor', axis=0, tiled=True)  29.8 us
  transfers between devices with their start and end apart: 50, of which 25 were waited for; matrix products, arithmetic and copies ran while one was open for 30% of the time, Pallas kernels for 0%

profile of v1, /device:TPU:0, one launch (start us, length us, event | category | flops | bytes accessed | tf_op | source)
XLA Modules:
  0.0 664.3 jit_solution(7864806715667158447)
XLA Ops:
  13.2 47.5 %all-gather.5.cloned.1.call-done = bf16[512,2048]{1,0:T(8,128)(2,1)} async-done(((bf16[128,2048]{1,0:T(8,128)(2,1)}), bf16[512,2048]{1,0:T(8,128)(2,1)}) %all-gather.5.cloned.1.call-update) | async-done | bytes 2097168 | tf_op jit(solution)/shard_map/all_gather | solution.py:157
  60.8 3.7 fusion.28
  64.5 2.9 fusion.31
  71.6 4.0 fusion.34
  81.7 42.4 %reduce-scatter.5.cloned.1.call-done = bf16[128,2048]{1,0:T(8,128)(2,1)} async-done(((bf16[512,2048]{1,0:T(8,128)(2,1)}), bf16[128,2048]{1,0:T(8,128)(2,1)}) %reduce-scatter.5.cloned.1.call-update) | async-done | bytes 524304 | tf_op jit(solution)/shard_map/reduce_scatter | solution.py:127
  129.0 44.4 %all-gather.7.cloned.1.call-done = bf16[512,2048]{1,0:T(8,128)(2,1)} async-done(((bf16[128,2048]{1,0:T(8,128)(2,1)}), bf16[512,2048]{1,0:T(8,128)(2,1)}) %all-gather.7.cloned.1.call-update) | async-done | bytes 2097168 | tf_op jit(solution)/shard_map/all_gather | solution.py:180
  173.4 8.4 %fusion.186 = f32[512,1408]{1,0:T(8,128)} fusion(bf16[512,2048]{1,0:T(8,128)(2,1)} %all-gather.7.cloned.1.call-done, bf16[2048,1408]{1,0:T(8,128)(2,1)} %param.20), kind=kOutput, calls=%fused_computation.283 | convolution fusion | flops 2952790016 | bytes 10747904 | tf_op jit(solution)/shard_map/dot_general | solution.py:181
  181.8 7.7 %fusion.187 = f32[512,1408]{1,0:T(8,128)} fusion(bf16[512,2048]{1,0:T(8,128)(2,1)S(1)} %copy-done.55, bf16[2048,1408]{1,0:T(8,128)(2,1)} %param.21), kind=kOutput, calls=%fused_computation.284 | convolution fusion | flops 2952790016 | bytes 10747904 | tf_op jit(solution)/shard_map/dot_general | solution.py:182
  189.5 29.8 %all-gather.9.cloned.1.call-done = bf16[512,2048]{1,0:T(8,128)(2,1)} async-done(((bf16[128,2048]{1,0:T(8,128)(2,1)}), bf16[512,2048]{1,0:T(8,128)(2,1)}) %all-gather.9.cloned.1.call-update) | async-done | bytes 2097168 | tf_op jit(solution)/shard_map/all_gather | solution.py:187
  219.3 10.4 %multiply_convert_fusion.1 = (bf16[512,1408]{1,0:T(8,128)(2,1)S(1)}, bf16[512,1408]{1,0:T(8,128)(2,1)S(1)}, bf16[512,1408]{1,0:T(8,128)(2,1)}) fusion(f32[512,1408]{1,0:T(8,128)} %fusion.186, f32[512,1408]{1,0:T(8,128)} %fusion.187, bf16[512,2048]{1,0:T(8,128)(2,1)} %all-gather.9.cloned.1.call-done, bf16[1408,2048]{1,0:T(8,128)(2,1)} %param.22), kind=kOutput, calls=%fused_computation.23 | convolution fusion | flops 2964324352 | bytes 17956864 | tf_op jit(solution)/shard_map/dot_general | solution.py:58
  229.7 6.5 fusion.188
  236.3 7.4 %add_convert_fusion.1 = bf16[512,2048]{1,0:T(8,128)(2,1)} fusion(f32[512,2048]{1,0:T(8,128)S(1)} %fusion.188, bf16[512,1408]{1,0:T(8,128)(2,1)S(1)} %get-tuple-element.38, bf16[2048,1408]{1,0:T(8,128)(2,1)} %param.21), kind=kOutput, calls=%fused_computation.14 | convolution fusion | flops 2954887168 | bytes 13500416 | tf_op jit(solution)/shard_map/dot_general | solution.py:58
  244.2 5.2 convolution_convert_fusion.1
  249.5 3.5 convolution_convert_fusion
  253.4 3.5 convolution_convert_fusion.2
  256.9 29.4 %reduce-scatter.9.cloned.1.call-done = bf16[128,2048]{1,0:T(8,128)(2,1)} async-done(((bf16[512,2048]{1,0:T(8,128)(2,1)}), bf16[128,2048]{1,0:T(8,128)(2,1)}) %reduce-scatter.9.cloned.1.call-update) | async-done | bytes 524304 | tf_op jit(solution)/shard_map/reduce_scatter | solution.py:127
  289.6 2.6 fusion.181
  292.6 3.6 fusion.101
  296.3 3.6 add_convert_fusion.4
  301.3 3.5 add_convert_fusion.3
  305.6 3.7 add_convert_fusion.2
  310.5 26.7 %all-gather.11.cloned.1.call-done = bf16[512,2048]{1,0:T(8,128)(2,1)} async-done(((bf16[128,2048]{1,0:T(8,128)(2,1)}), bf16[512,2048]{1,0:T(8,128)(2,1)}) %all-gather.11.cloned.1.call-update) | async-done | bytes 2097168 | tf_op jit(solution)/shard_map/all_gather | solution.py:206
  337.2 3.0 fusion.54
  340.3 5.7 multiply_convert_fusion
  355.6 2.8 add_convert_fusion
  383.7 2.7 constant_dynamic-update-slice_fusion.3
  390.4 2.8 constant_dynamic-update-slice_fusion.13
  400.4 10.4 %collective-permute-done.33 = bf16[256,1408]{1,0:T(8,128)(2,1)S(1)} collective-permute-done((bf16[256,1408]{1,0:T(8,128)(2,1)S(1)}, bf16[256,1408]{1,0:T(8,128)(2,1)S(1)}, u32[]{:S(2)}, u32[]{:S(2)}) %collective-permute-start.33) | collective-permute-done | bytes 720928 | tf_op jit(solution)/shard_map/ppermute | solution.py:92
  413.2 5.0 convolution_convert_fusion.4
  418.2 8.1 %collective-permute-done.39 = bf16[176,2048]{1,0:T(8,128)(2,1)} collective-permute-done((bf16[176,2048]{1,0:T(8,128)(2,1)}, bf16[176,2048]{1,0:T(8,128)(2,1)}, u32[]{:S(2)}, u32[]{:S(2)}) %collective-permute-start.39) | collective-permute-done | bytes 720928 | tf_op jit(solution)/shard_map/ppermute | solution.py:92
  444.7 5.4 broadcast.153.clone
  450.1 4.7 convert_dynamic-update-slice_fusion.5
  463.3 2.7 convert_dynamic-update-slice_fusion.1
  475.4 2.7 convolution_convert_fusion.5
  484.6 15.2 %psum.37 = f32[3,512]{1,0:T(4,128)} all-reduce(f32[3,512]{1,0:T(4,128)S(1)} %pad_maximum_fusion.11), channel_id=1, replica_groups=mesh['dp'=8,'tensor'=4] {'dp'}, use_global_device_ids=true, to_apply=%region_21.22 | all-reduce | flops 1536 | bytes 12288 | tf_op jit(solution)/shard_map/psum | solution.py:252
  513.7 4.3 collective-permute-done.7
  519.9 6.5 collective-permute-done.1
  528.3 6.5 collective-permute-done.19
  549.7 5.5 collective-permute-done.3
  555.3 5.6 collective-permute-done.21
  566.2 3.8 collective-permute-done.4
  580.8 2.6 broadcast_in_dim.24
  585.0 5.2 convert_dynamic-update-slice_fusion.4
  593.6 4.7 convert_dynamic-update-slice_fusion
  604.5 2.8 convert_dynamic-update-slice_fusion.12
  607.4 5.4 pad_maximum_fusion
  614.3 39.1 %all-reduce = (f32[2048]{0:T(1024)}, f32[2048]{0:T(1024)}, f32[2048]{0:T(1024)}, f32[2048]{0:T(1024)}) all-reduce(f32[2048]{0:T(1024)S(1)} %get-tuple-element.14, f32[2048]{0:T(1024)S(1)} %get-tuple-element.19, f32[2048]{0:T(1024)S(1)} %get-tuple-element.12, f32[2048]{0:T(1024)S(1)} %copy-done.68), channel_id=1, replica_groups=mesh['dp'=8,'tensor'=4] {'dp','tensor'}, use_global_device_ids=true, to_apply=%region_15.16 | all-reduce | flops 8192 | bytes 65536 | tf_op jit(solution)/shard_map/psum | solution.py:249
  653.5 3.8 fusion.45
  (419 shorter events, 180.3 us)
Async XLA Ops:
  7.2 53.6 %all-gather.5.cloned.1.call-start = ((), (), s32[]{:S(2)}) async-start(), calls=%async_computation.4 | async-start | bytes 2621440 | tf_op jit(solution)/shard_map/all_gather | solution.py:157
  12.2 111.8 %reduce-scatter.5.cloned.1.call-start = ((), (), s32[]{:S(2)}) async-start(), calls=%async_computation.5 | async-start | bytes 2621440 | tf_op jit(solution)/shard_map/reduce_scatter | solution.py:127
  81.4 92.0 %all-gather.7.cloned.1.call-start = ((), (), s32[]{:S(2)}) async-start(), calls=%async_computation.6 | async-start | bytes 2621440 | tf_op jit(solution)/shard_map/all_gather | solution.py:180
  128.4 90.9 %all-gather.9.cloned.1.call-start = ((), (), s32[]{:S(2)}) async-start(), calls=%async_computation.8 | async-start | bytes 2621440 | tf_op jit(solution)/shard_map/all_gather | solution.py:187
  129.0 157.3 %reduce-scatter.9.cloned.1.call-start = ((), (), s32[]{:S(2)}) async-start(), calls=%async_computation.9 | async-start | bytes 2621440 | tf_op jit(solution)/shard_map/reduce_scatter | solution.py:127
  243.7 93.5 %all-gather.11.cloned.1.call-start = ((), (), s32[]{:S(2)}) async-start(), calls=%async_computation.10 | async-start | bytes 2621440 | tf_op jit(solution)/shard_map/all_gather | solution.py:206
  249.5 46.8 %collective-permute-start.24 = (bf16[1024,1408]{1,0:T(8,128)(2,1)}, bf16[1024,1408]{1,0:T(8,128)(2,1)}, u32[]{:S(2)}, u32[]{:S(2)}) collective-permute-start(bf16[1024,1408]{1,0:T(8,128)(2,1)} %convolution_convert_fusion.1), channel_id=1, source_target_pairs={{0,4},{4,0},{8,12},{12,8},{16,20},{20,16},{24,28},{28,24},{1,5},{5... | collective-permute-start | bytes 8650760 | tf_op jit(solution)/shard_map/ppermute | solution.py:92
  252.9 48.4 %collective-permute-start.30 = (bf16[1024,1408]{1,0:T(8,128)(2,1)}, bf16[1024,1408]{1,0:T(8,128)(2,1)}, u32[]{:S(2)}, u32[]{:S(2)}) collective-permute-start(bf16[1024,1408]{1,0:T(8,128)(2,1)} %convolution_convert_fusion), channel_id=1, source_target_pairs={{0,4},{4,0},{8,12},{12,8},{16,20},{20,16},{24,28},{28,24},{1,5},{5... | collective-permute-start | bytes 8650760 | tf_op jit(solution)/shard_map/ppermute | solution.py:92
  256.9 48.7 %collective-permute-start.36 = (bf16[704,2048]{1,0:T(8,128)(2,1)}, bf16[704,2048]{1,0:T(8,128)(2,1)}, u32[]{:S(2)}, u32[]{:S(2)}) collective-permute-start(bf16[704,2048]{1,0:T(8,128)(2,1)} %convolution_convert_fusion.2), channel_id=1, source_target_pairs={{0,4},{4,0},{8,12},{12,8},{16,20},{20,16},{24,28},{28,24},{1,5},{5... | collective-permute-start | bytes 8650760 | tf_op jit(solution)/shard_map/ppermute | solution.py:92
  292.2 320.5 %reduce-scatter.11.cloned.1.call-start = ((), (), s32[]{:S(2)}) async-start(), calls=%async_computation.11 | async-start | bytes 2621440 | tf_op jit(solution)/shard_map/reduce_scatter | solution.py:127
  299.9 61.4 %collective-permute-start.25 = (bf16[512,1408]{1,0:T(8,128)(2,1)}, bf16[512,1408]{1,0:T(8,128)(2,1)}, u32[]{:S(2)}, u32[]{:S(2)}) collective-permute-start(bf16[512,1408]{1,0:T(8,128)(2,1)} %add_convert_fusion.4), channel_id=1, source_target_pairs={{0,8},{4,20},{8,0},{12,28},{16,24},{20,4},{24,16},{28,12},{1,9},{5... | collective-permute-start | bytes 4325384 | tf_op jit(solution)/shard_map/ppermute | solution.py:92
  304.8 61.7 %collective-permute-start.31 = (bf16[512,1408]{1,0:T(8,128)(2,1)}, bf16[512,1408]{1,0:T(8,128)(2,1)}, u32[]{:S(2)}, u32[]{:S(2)}) collective-permute-start(bf16[512,1408]{1,0:T(8,128)(2,1)} %add_convert_fusion.3), channel_id=1, source_target_pairs={{0,8},{4,20},{8,0},{12,28},{16,24},{20,4},{24,16},{28,12},{1,9},{5... | collective-permute-start | bytes 4325384 | tf_op jit(solution)/shard_map/ppermute | solution.py:92
  309.3 60.1 %collective-permute-start.37 = (bf16[352,2048]{1,0:T(8,128)(2,1)}, bf16[352,2048]{1,0:T(8,128)(2,1)}, u32[]{:S(2)}, u32[]{:S(2)}) collective-permute-start(bf16[352,2048]{1,0:T(8,128)(2,1)} %add_convert_fusion.2), channel_id=1, source_target_pairs={{0,8},{4,20},{8,0},{12,28},{16,24},{20,4},{24,16},{28,12},{1,9},{5... | collective-permute-start | bytes 4325384 | tf_op jit(solution)/shard_map/ppermute | solution.py:92
  358.4 295.0 %reduce-scatter.7.cloned.1.call-start = ((), (), s32[]{:S(2)}) async-start(), calls=%async_computation.7 | async-start | bytes 2621440 | tf_op jit(solution)/shard_map/reduce_scatter | solution.py:127
  363.5 11.4 %collective-permute-start.26 = (bf16[256,1408]{1,0:T(8,128)(2,1)S(1)}, bf16[256,1408]{1,0:T(8,128)(2,1)S(1)}, u32[]{:S(2)}, u32[]{:S(2)}) collective-permute-start(bf16[256,1408]{1,0:T(8,128)(2,1)S(1)} %add_convert_fusion.10), channel_id=1, source_target_pairs={{0,16},{4,12},{8,24},{12,4},{16,0},{20,28},{24,8},{28,20},{1,17},{... | collective-permute-start | bytes 2162696 | tf_op jit(solution)/shard_map/ppermute | solution.py:92
  368.8 13.8 %collective-permute-start.32 = (bf16[256,1408]{1,0:T(8,128)(2,1)S(1)}, bf16[256,1408]{1,0:T(8,128)(2,1)S(1)}, u32[]{:S(2)}, u32[]{:S(2)}) collective-permute-start(bf16[256,1408]{1,0:T(8,128)(2,1)S(1)} %add_convert_fusion.8), channel_id=1, source_target_pairs={{0,16},{4,12},{8,24},{12,4},{16,0},{20,28},{24,8},{28,20},{1,17},{... | collective-permute-start | bytes 2162696 | tf_op jit(solution)/shard_map/ppermute | solution.py:92
  371.5 18.8 %collective-permute-start.38 = (bf16[176,2048]{1,0:T(8,128)(2,1)S(1)}, bf16[176,2048]{1,0:T(8,128)(2,1)S(1)}, u32[]{:S(2)}, u32[]{:S(2)}) collective-permute-start(bf16[176,2048]{1,0:T(8,128)(2,1)S(1)} %add_convert_fusion.6), channel_id=1, source_target_pairs={{0,16},{4,12},{8,24},{12,4},{16,0},{20,28},{24,8},{28,20},{1,17},{... | collective-permute-start | bytes 2162696 | tf_op jit(solution)/shard_map/ppermute | solution.py:92
  378.5 19.4 %collective-permute-start.27 = (bf16[256,1408]{1,0:T(8,128)(2,1)S(1)}, bf16[256,1408]{1,0:T(8,128)(2,1)S(1)}, u32[]{:S(2)}, u32[]{:S(2)}) collective-permute-start(bf16[256,1408]{1,0:T(8,128)(2,1)S(1)} %get-tuple-element.29), channel_id=1, source_target_pairs={{0,16},{4,12},{8,24},{12,4},{16,0},{20,28},{24,8},{28,20},{1,17},{... | collective-permute-start | bytes 2162696 | tf_op jit(solution)/shard_map/ppermute | solution.py:92
  386.4 24.4 %collective-permute-start.33 = (bf16[256,1408]{1,0:T(8,128)(2,1)S(1)}, bf16[256,1408]{1,0:T(8,128)(2,1)S(1)}, u32[]{:S(2)}, u32[]{:S(2)}) collective-permute-start(bf16[256,1408]{1,0:T(8,128)(2,1)S(1)} %get-tuple-element.27), channel_id=1, source_target_pairs={{0,16},{4,12},{8,24},{12,4},{16,0},{20,28},{24,8},{28,20},{1,17},{... | collective-permute-start | bytes 2162696 | tf_op jit(solution)/shard_map/ppermute | solution.py:92
  394.3 32.0 %collective-permute-start.39 = (bf16[176,2048]{1,0:T(8,128)(2,1)}, bf16[176,2048]{1,0:T(8,128)(2,1)}, u32[]{:S(2)}, u32[]{:S(2)}) collective-permute-start(bf16[176,2048]{1,0:T(8,128)(2,1)} %get-tuple-element.25), channel_id=1, source_target_pairs={{0,16},{4,12},{8,24},{12,4},{16,0},{20,28},{24,8},{28,20},{1,17},{... | collective-permute-start | bytes 2162696 | tf_op jit(solution)/shard_map/ppermute | solution.py:92
  398.9 39.5 %collective-permute-start.28 = (bf16[512,1408]{1,0:T(8,128)(2,1)}, bf16[512,1408]{1,0:T(8,128)(2,1)}, u32[]{:S(2)}, u32[]{:S(2)}) collective-permute-start(bf16[512,1408]{1,0:T(8,128)(2,1)} %constant_dynamic-update-slice_fusion.6), channel_id=1, source_target_pairs={{0,8},{4,20},{8,0},{12,28},{16,24},{20,4},{24,16},{28,12},{1,9},{5... | collective-permute-start | bytes 4325384 | tf_op jit(solution)/shard_map/ppermute | solution.py:92
  411.7 31.4 %collective-permute-start.34 = (bf16[512,1408]{1,0:T(8,128)(2,1)}, bf16[512,1408]{1,0:T(8,128)(2,1)}, u32[]{:S(2)}, u32[]{:S(2)}) collective-permute-start(bf16[512,1408]{1,0:T(8,128)(2,1)} %constant_dynamic-update-slice_fusion.2), channel_id=1, source_target_pairs={{0,8},{4,20},{8,0},{12,28},{16,24},{20,4},{24,16},{28,12},{1,9},{5... | collective-permute-start | bytes 4325384 | tf_op jit(solution)/shard_map/ppermute | solution.py:92
  427.5 30.9 %collective-permute-start.40 = (bf16[352,2048]{1,0:T(8,128)(2,1)S(1)}, bf16[352,2048]{1,0:T(8,128)(2,1)S(1)}, u32[]{:S(2)}, u32[]{:S(2)}) collective-permute-start(bf16[352,2048]{1,0:T(8,128)(2,1)S(1)} %constant_dynamic-update-slice_fusion.22), channel_id=1, source_target_pairs={{0,8},{4,20},{8,0},{12,28},{16,24},{20,4},{24,16},{28,12},{1,9},{5... | collective-permute-start | bytes 4325384 | tf_op jit(solution)/shard_map/ppermute | solution.py:92
  441.0 144.0 %collective-permute-start.29 = (bf16[1024,1408]{1,0:T(8,128)(2,1)}, bf16[1024,1408]{1,0:T(8,128)(2,1)}, u32[]{:S(2)}, u32[]{:S(2)}) collective-permute-start(bf16[1024,1408]{1,0:T(8,128)(2,1)} %constant_dynamic-update-slice_fusion.4), channel_id=1, source_target_pairs={{0,4},{4,0},{8,12},{12,8},{16,20},{20,16},{24,28},{28,24},{1,5},{5... | collective-permute-start | bytes 8650760 | tf_op jit(solution)/shard_map/ppermute | solution.py:92
  469.8 31.5 %collective-permute-start.12 = (bf16[1024,512]{1,0:T(8,128)(2,1)}, bf16[1024,512]{1,0:T(8,128)(2,1)}, u32[]{:S(2)}, u32[]{:S(2)}) collective-permute-start(bf16[1024,512]{1,0:T(8,128)(2,1)} %convolution_convert_fusion.6), channel_id=1, source_target_pairs={{0,4},{4,0},{8,12},{12,8},{16,20},{20,16},{24,28},{28,24},{1,5},{5... | collective-permute-start | bytes 3145736 | tf_op jit(solution)/shard_map/ppermute | solution.py:92
  472.9 30.2 %collective-permute-start.6 = (bf16[1024,512]{1,0:T(8,128)(2,1)}, bf16[1024,512]{1,0:T(8,128)(2,1)}, u32[]{:S(2)}, u32[]{:S(2)}) collective-permute-start(bf16[1024,512]{1,0:T(8,128)(2,1)} %convolution_convert_fusion.7), channel_id=1, source_target_pairs={{0,4},{4,0},{8,12},{12,8},{16,20},{20,16},{24,28},{28,24},{1,5},{5... | collective-permute-start | bytes 3145736 | tf_op jit(solution)/shard_map/ppermute | solution.py:92
  474.7 30.1 %collective-permute-start = (bf16[1024,512]{1,0:T(8,128)(2,1)}, bf16[1024,512]{1,0:T(8,128)(2,1)}, u32[]{:S(2)}, u32[]{:S(2)}) collective-permute-start(bf16[1024,512]{1,0:T(8,128)(2,1)} %convolution_convert_fusion.8), channel_id=1, source_target_pairs={{0,4},{4,0},{8,12},{12,8},{16,20},{20,16},{24,28},{28,24},{1,5},{5... | collective-permute-start | bytes 3145736 | tf_op jit(solution)/shard_map/ppermute | solution.py:92
  478.2 30.2 %collective-permute-start.18 = (bf16[256,2048]{1,0:T(8,128)(2,1)}, bf16[256,2048]{1,0:T(8,128)(2,1)}, u32[]{:S(2)}, u32[]{:S(2)}) collective-permute-start(bf16[256,2048]{1,0:T(8,128)(2,1)} %convolution_convert_fusion.5), channel_id=1, source_target_pairs={{0,4},{4,0},{8,12},{12,8},{16,20},{20,16},{24,28},{28,24},{1,5},{5... | collective-permute-start | bytes 3145736 | tf_op jit(solution)/shard_map/ppermute | solution.py:92
  501.3 89.0 %collective-permute-start.35 = (bf16[1024,1408]{1,0:T(8,128)(2,1)}, bf16[1024,1408]{1,0:T(8,128)(2,1)}, u32[]{:S(2)}, u32[]{:S(2)}) collective-permute-start(bf16[1024,1408]{1,0:T(8,128)(2,1)} %copy-done.20), channel_id=1, source_target_pairs={{0,4},{4,0},{8,12},{12,8},{16,20},{20,16},{24,28},{28,24},{1,5},{5... | collective-permute-start | bytes 8650760 | tf_op jit(solution)/shard_map/ppermute | solution.py:92
  503.1 9.2 %collective-permute-start.13 = (bf16[512,512]{1,0:T(8,128)(2,1)S(1)}, bf16[512,512]{1,0:T(8,128)(2,1)S(1)}, u32[]{:S(2)}, u32[]{:S(2)}) collective-permute-start(bf16[512,512]{1,0:T(8,128)(2,1)S(1)} %add_convert_fusion.12), channel_id=1, source_target_pairs={{0,8},{4,20},{8,0},{12,28},{16,24},{20,4},{24,16},{28,12},{1,9},{5... | collective-permute-start | bytes 1572872 | tf_op jit(solution)/shard_map/ppermute | solution.py:92
  504.8 13.2 %collective-permute-start.7 = (bf16[512,512]{1,0:T(8,128)(2,1)S(1)}, bf16[512,512]{1,0:T(8,128)(2,1)S(1)}, u32[]{:S(2)}, u32[]{:S(2)}) collective-permute-start(bf16[512,512]{1,0:T(8,128)(2,1)S(1)} %add_convert_fusion.13), channel_id=1, source_target_pairs={{0,8},{4,20},{8,0},{12,28},{16,24},{20,4},{24,16},{28,12},{1,9},{5... | collective-permute-start | bytes 1572872 | tf_op jit(solution)/shard_map/ppermute | solution.py:92
  508.4 18.0 %collective-permute-start.1 = (bf16[512,512]{1,0:T(8,128)(2,1)S(1)}, bf16[512,512]{1,0:T(8,128)(2,1)S(1)}, u32[]{:S(2)}, u32[]{:S(2)}) collective-permute-start(bf16[512,512]{1,0:T(8,128)(2,1)S(1)} %add_convert_fusion.14), channel_id=1, source_target_pairs={{0,8},{4,20},{8,0},{12,28},{16,24},{20,4},{24,16},{28,12},{1,9},{5... | collective-permute-start | bytes 1572872 | tf_op jit(solution)/shard_map/ppermute | solution.py:92
  512.4 22.5 %collective-permute-start.19 = (bf16[128,2048]{1,0:T(8,128)(2,1)S(1)}, bf16[128,2048]{1,0:T(8,128)(2,1)S(1)}, u32[]{:S(2)}, u32[]{:S(2)}) collective-permute-start(bf16[128,2048]{1,0:T(8,128)(2,1)S(1)} %add_convert_fusion.11), channel_id=1, source_target_pairs={{0,8},{4,20},{8,0},{12,28},{16,24},{20,4},{24,16},{28,12},{1,9},{5... | collective-permute-start | bytes 1572872 | tf_op jit(solution)/shard_map/ppermute | solution.py:92
  518.0 18.9 %collective-permute-start.14 = (bf16[256,512]{1,0:T(8,128)(2,1)S(1)}, bf16[256,512]{1,0:T(8,128)(2,1)S(1)}, u32[]{:S(2)}, u32[]{:S(2)}) collective-permute-start(bf16[256,512]{1,0:T(8,128)(2,1)S(1)} %add_convert_fusion.20), channel_id=1, source_target_pairs={{0,16},{4,12},{8,24},{12,4},{16,0},{20,28},{24,8},{28,20},{1,17},{... | collective-permute-start | bytes 786440 | tf_op jit(solution)/shard_map/ppermute | solution.py:92
  526.4 13.2 %collective-permute-start.8 = (bf16[256,512]{1,0:T(8,128)(2,1)S(1)}, bf16[256,512]{1,0:T(8,128)(2,1)S(1)}, u32[]{:S(2)}, u32[]{:S(2)}) collective-permute-start(bf16[256,512]{1,0:T(8,128)(2,1)S(1)} %add_convert_fusion.22), channel_id=1, source_target_pairs={{0,16},{4,12},{8,24},{12,4},{16,0},{20,28},{24,8},{28,20},{1,17},{... | collective-permute-start | bytes 786440 | tf_op jit(solution)/shard_map/ppermute | solution.py:92
  536.9 7.2 %collective-permute-start.20 = (bf16[64,2048]{1,0:T(8,128)(2,1)S(1)}, bf16[64,2048]{1,0:T(8,128)(2,1)S(1)}, u32[]{:S(2)}, u32[]{:S(2)}) collective-permute-start(bf16[64,2048]{1,0:T(8,128)(2,1)S(1)} %add_convert_fusion.18), channel_id=1, source_target_pairs={{0,16},{4,12},{8,24},{12,4},{16,0},{20,28},{24,8},{28,20},{1,17},{... | collective-permute-start | bytes 786440 | tf_op jit(solution)/shard_map/ppermute | solution.py:92
  541.5 8.2 %collective-permute-start.9 = (bf16[256,512]{1,0:T(8,128)(2,1)S(1)}, bf16[256,512]{1,0:T(8,128)(2,1)S(1)}, u32[]{:S(2)}, u32[]{:S(2)}) collective-permute-start(bf16[256,512]{1,0:T(8,128)(2,1)S(1)} %get-tuple-element.35), channel_id=1, source_target_pairs={{0,16},{4,12},{8,24},{12,4},{16,0},{20,28},{24,8},{28,20},{1,17},{... | collective-permute-start | bytes 786440 | tf_op jit(solution)/shard_map/ppermute | solution.py:92
  544.2 11.1 %collective-permute-start.3 = (bf16[256,512]{1,0:T(8,128)(2,1)S(1)}, bf16[256,512]{1,0:T(8,128)(2,1)S(1)}, u32[]{:S(2)}, u32[]{:S(2)}) collective-permute-start(bf16[256,512]{1,0:T(8,128)(2,1)S(1)} %get-tuple-element.33), channel_id=1, source_target_pairs={{0,16},{4,12},{8,24},{12,4},{16,0},{20,28},{24,8},{28,20},{1,17},{... | collective-permute-start | bytes 786440 | tf_op jit(solution)/shard_map/ppermute | solution.py:92
  546.8 14.0 %collective-permute-start.21 = (bf16[64,2048]{1,0:T(8,128)(2,1)S(1)}, bf16[64,2048]{1,0:T(8,128)(2,1)S(1)}, u32[]{:S(2)}, u32[]{:S(2)}) collective-permute-start(bf16[64,2048]{1,0:T(8,128)(2,1)S(1)} %get-tuple-element.31), channel_id=1, source_target_pairs={{0,16},{4,12},{8,24},{12,4},{16,0},{20,28},{24,8},{28,20},{1,17},{... | collective-permute-start | bytes 786440 | tf_op jit(solution)/shard_map/ppermute | solution.py:92
  549.7 13.5 %collective-permute-start.16 = (bf16[512,512]{1,0:T(8,128)(2,1)S(1)}, bf16[512,512]{1,0:T(8,128)(2,1)S(1)}, u32[]{:S(2)}, u32[]{:S(2)}) collective-permute-start(bf16[512,512]{1,0:T(8,128)(2,1)S(1)} %constant_dynamic-update-slice_fusion.16), channel_id=1, source_target_pairs={{0,8},{4,20},{8,0},{12,28},{16,24},{20,4},{24,16},{28,12},{1,9},{5... | collective-permute-start | bytes 1572872 | tf_op jit(solution)/shard_map/ppermute | solution.py:92
  555.2 9.2 %collective-permute-start.10 = (bf16[512,512]{1,0:T(8,128)(2,1)S(1)}, bf16[512,512]{1,0:T(8,128)(2,1)S(1)}, u32[]{:S(2)}, u32[]{:S(2)}) collective-permute-start(bf16[512,512]{1,0:T(8,128)(2,1)S(1)} %constant_dynamic-update-slice_fusion.20), channel_id=1, source_target_pairs={{0,8},{4,20},{8,0},{12,28},{16,24},{20,4},{24,16},{28,12},{1,9},{5... | collective-permute-start | bytes 1572872 | tf_op jit(solution)/shard_map/ppermute | solution.py:92
  560.8 9.2 %collective-permute-start.4 = (bf16[512,512]{1,0:T(8,128)(2,1)S(1)}, bf16[512,512]{1,0:T(8,128)(2,1)S(1)}, u32[]{:S(2)}, u32[]{:S(2)}) collective-permute-start(bf16[512,512]{1,0:T(8,128)(2,1)S(1)} %constant_dynamic-update-slice_fusion.25), channel_id=1, source_target_pairs={{0,8},{4,20},{8,0},{12,28},{16,24},{20,4},{24,16},{28,12},{1,9},{5... | collective-permute-start | bytes 1572872 | tf_op jit(solution)/shard_map/ppermute | solution.py:92
  563.2 30.4 %collective-permute-start.41 = (bf16[704,2048]{1,0:T(8,128)(2,1)}, bf16[704,2048]{1,0:T(8,128)(2,1)}, u32[]{:S(2)}, u32[]{:S(2)}) collective-permute-start(bf16[704,2048]{1,0:T(8,128)(2,1)} %constant_dynamic-update-slice_fusion.8), channel_id=1, source_target_pairs={{0,4},{4,0},{8,12},{12,8},{16,20},{20,16},{24,28},{28,24},{1,5},{5... | collective-permute-start | bytes 8650760 | tf_op jit(solution)/shard_map/ppermute | solution.py:92
  564.5 11.2 %collective-permute-start.22 = (bf16[128,2048]{1,0:T(8,128)(2,1)S(1)}, bf16[128,2048]{1,0:T(8,128)(2,1)S(1)}, u32[]{:S(2)}, u32[]{:S(2)}) collective-permute-start(bf16[128,2048]{1,0:T(8,128)(2,1)S(1)} %constant_dynamic-update-slice_fusion.11), channel_id=1, source_target_pairs={{0,8},{4,20},{8,0},{12,28},{16,24},{20,4},{24,16},{28,12},{1,9},{5... | collective-permute-start | bytes 1572872 | tf_op jit(solution)/shard_map/ppermute | solution.py:92
  570.1 28.2 %collective-permute-start.17 = (bf16[1024,512]{1,0:T(8,128)(2,1)S(1)}, bf16[1024,512]{1,0:T(8,128)(2,1)}, u32[]{:S(2)}, u32[]{:S(2)}) collective-permute-start(bf16[1024,512]{1,0:T(8,128)(2,1)S(1)} %constant_dynamic-update-slice_fusion.14), channel_id=1, source_target_pairs={{0,4},{4,0},{8,12},{12,8},{16,20},{20,16},{24,28},{28,24},{1,5},{5... | collective-permute-start | bytes 3145736 | tf_op jit(solution)/shard_map/ppermute | solution.py:92
  575.7 24.9 %collective-permute-start.11 = (bf16[1024,512]{1,0:T(8,128)(2,1)}, bf16[1024,512]{1,0:T(8,128)(2,1)}, u32[]{:S(2)}, u32[]{:S(2)}) collective-permute-start(bf16[1024,512]{1,0:T(8,128)(2,1)} %constant_dynamic-update-slice_fusion.18), channel_id=1, source_target_pairs={{0,4},{4,0},{8,12},{12,8},{16,20},{20,16},{24,28},{28,24},{1,5},{5... | collective-permute-start | bytes 3145736 | tf_op jit(solution)/shard_map/ppermute | solution.py:92
  585.0 17.9 %collective-permute-start.5 = (bf16[1024,512]{1,0:T(8,128)(2,1)S(1)}, bf16[1024,512]{1,0:T(8,128)(2,1)}, u32[]{:S(2)}, u32[]{:S(2)}) collective-permute-start(bf16[1024,512]{1,0:T(8,128)(2,1)S(1)} %constant_dynamic-update-slice_fusion.23), channel_id=1, source_target_pairs={{0,4},{4,0},{8,12},{12,8},{16,20},{20,16},{24,28},{28,24},{1,5},{5... | collective-permute-start | bytes 3145736 | tf_op jit(solution)/shard_map/ppermute | solution.py:92
  590.2 14.2 %collective-permute-start.23 = (bf16[256,2048]{1,0:T(8,128)(2,1)S(1)}, bf16[256,2048]{1,0:T(8,128)(2,1)}, u32[]{:S(2)}, u32[]{:S(2)}) collective-permute-start(bf16[256,2048]{1,0:T(8,128)(2,1)S(1)} %constant_dynamic-update-slice_fusion.9), channel_id=1, source_target_pairs={{0,4},{4,0},{8,12},{12,8},{16,20},{20,16},{24,28},{28,24},{1,5},{5... | collective-permute-start | bytes 3145736 | tf_op jit(solution)/shard_map/ppermute | solution.py:92
  (101 other events, 893.3 us)
Sparse Core Ops, SparseCore 0:
  12.4 48.3 all-gather.4
  81.6 42.4 reduce-scatter.4
  128.5 44.8 all-gather.6
  174.8 44.4 all-gather.8
  243.8 42.4 reduce-scatter.8
  292.3 44.8 all-gather.10
  358.5 42.4 reduce-scatter.10
  418.3 41.5 reduce-scatter.6

commit v2 on v1

--- a/solution.py
+++ b/solution.py
@@ -3,6 +3,8 @@
 import jax
 import jax.numpy as jnp
 from jax import lax
+from jax.experimental import pallas as pl
+from jax.experimental.pallas import tpu as pltpu
 from jax.sharding import PartitionSpec as P
 
 HD = 64
@@ -129,8 +131,447 @@
     ).astype(jnp.float32)
 
 
+MESH = pl.DeviceIdType.MESH
+
+
+def line_barrier(place, ways):
+    barrier = pltpu.get_barrier_semaphore()
+    for step, there in ((-1, place > 0), (1, place < ways - 1)):
+
+        @pl.when(there)
+        def _():
+            pl.semaphore_signal(
+                barrier, inc=1, device_id={"tensor": place + step}, device_id_type=MESH
+            )
+
+    pl.semaphore_wait(barrier, (place > 0).astype(jnp.int32) + (place < ways - 1).astype(jnp.int32))
+
+
+class LineGather:
+    def __init__(self, rows, place, ways, send_sem, recv_sem):
+        self.rows, self.place, self.ways = rows, place, ways
+        self.send_sem, self.recv_sem = send_sem, recv_sem
+        self.size = rows.shape[0] // ways
+
+    def view(self, slot):
+        return self.rows.at[pl.ds(pl.multiple_of(slot * self.size, self.size), self.size)]
+
+    def copy(self, slot, way):
+        return pltpu.make_async_remote_copy(
+            src_ref=self.view(slot),
+            dst_ref=self.view(slot),
+            send_sem=self.send_sem.at[way, slot],
+            recv_sem=self.recv_sem.at[slot],
+            device_id={"tensor": self.place + 1 - 2 * way},
+            device_id_type=MESH,
+        )
+
+    def start(self):
+        @pl.when(self.place < self.ways - 1)
+        def _():
+            self.copy(self.place, 0).start()
+
+        @pl.when(self.place > 0)
+        def _():
+            self.copy(self.place, 1).start()
+
+    def hop(self, step):
+        before, after = self.place - step, self.place + step
+
+        @pl.when(before >= 0)
+        def _():
+            self.copy(before, 0).wait_recv()
+
+            @pl.when(self.place < self.ways - 1)
+            def _():
+                self.copy(before, 0).start()
+
+        @pl.when(after < self.ways)
+        def _():
+            self.copy(after, 1).wait_recv()
+
+            @pl.when(self.place > 0)
+            def _():
+                self.copy(after, 1).start()
+
+    def drain(self):
+        def one(slot, carry):
+            @pl.when((slot <= self.place) & (self.place < self.ways - 1))
+            def _():
+                self.copy(slot, 0).wait_send()
+
+            @pl.when((slot >= self.place) & (self.place > 0))
+            def _():
+                self.copy(slot, 1).wait_send()
+
+            return carry
+
+        lax.fori_loop(0, self.ways, one, 0)
+
+    def each(self, work, hop=True):
+        def step_body(step, carry):
+            if hop:
+
+                @pl.when(step > 0)
+                def _():
+                    self.hop(step)
+
+            def side(which, inner_carry):
+                slot = jnp.where(which == 0, self.place - step, self.place + step)
+
+                @pl.when((slot >= 0) & (slot < self.ways) & ((which == 0) | (step > 0)))
+                def _():
+                    work(slot)
+
+                return inner_carry
+
+            return lax.fori_loop(0, 2, side, carry)
+
+        lax.fori_loop(0, self.ways, step_body, 0)
+
+
+class LineScatter:
+    def __init__(self, held, arrived, place, ways, send_sem, recv_sem):
+        self.held, self.arrived, self.place, self.ways = held, arrived, place, ways
+        self.send_sem, self.recv_sem = send_sem, recv_sem
+
+    def copy(self, way, slot):
+        return pltpu.make_async_remote_copy(
+            src_ref=self.held.at[slot],
+            dst_ref=self.arrived.at[way, slot],
+            send_sem=self.send_sem.at[slot],
+            recv_sem=self.recv_sem.at[way, slot],
+            device_id={"tensor": self.place + 1 - 2 * way},
+            device_id_type=MESH,
+        )
+
+    def has_source(self, way):
+        return jnp.where(way == 0, self.place > 0, self.place < self.ways - 1)
+
+    def send_all(self, partial, between=None):
+        def step_body(i, carry):
+            step = self.ways - 1 - i
+
+            def side(way, inner_carry):
+                slot = jnp.where(way == 0, self.place + step, self.place - step)
+
+                @pl.when((slot >= 0) & (slot < self.ways))
+                def _():
+                    self.held[slot] = partial(slot).astype(jnp.bfloat16)
+
+                    @pl.when(self.has_source(way))
+                    def _():
+                        self.copy(way, slot).wait_recv()
+                        self.held[slot] = (
+                            self.held[slot].astype(jnp.float32)
+                            + self.arrived[way, slot].astype(jnp.float32)
+                        ).astype(jnp.bfloat16)
+
+                    self.copy(way, slot).start()
+
+                return inner_carry
+
+            carry = lax.fori_loop(0, 2, side, carry)
+            if between is not None:
+                between(i)
+            return carry
+
+        lax.fori_loop(0, self.ways - 1, step_body, 0)
+
+    def finish(self, total):
+        for way in range(2):
+
+            @pl.when(self.has_source(way))
+            def _():
+                self.copy(way, self.place).wait_recv()
+                total[...] += self.arrived[way, self.place].astype(jnp.float32)
+
+    def drain(self):
+        def one(slot, carry):
+            for way, there in ((0, slot > self.place), (1, slot < self.place)):
+
+                @pl.when(there)
+                def _():
+                    self.copy(way, slot).wait_send()
+
+            return carry
+
+        lax.fori_loop(0, self.ways, one, 0)
+
+
+def norm_rows(values, gain, bias):
+    center = jnp.mean(values, axis=-1, keepdims=True)
+    offset = values - center
+    inverse = lax.rsqrt(jnp.mean(offset * offset, axis=-1, keepdims=True) + epsilon)
+    return offset * inverse * gain + bias
+
+
+def attention_tile(length, query, keys, values, mixed, logsum, base, tile):
+    columns = pl.ds(pl.multiple_of(tile * 128, 128), 128)
+    scale = HD ** (-0.5)
+    block = length // 2
+    for part in range(2):
+        first = part * block
+        span = first + block
+        rows = pl.ds(base + first, block)
+        past = pl.ds(base, span)
+        here = query[rows, columns]
+        lane = lax.broadcasted_iota(jnp.int32, here.shape, 1)
+        causal = (
+            lax.broadcasted_iota(jnp.int32, (block, span), 0) + first
+            >= lax.broadcasted_iota(jnp.int32, (block, span), 1)
+        )
+        sums = logsum[rows, :]
+        results = []
+        for head in range(2):
+            mine = (lane // HD) == head
+            scores = product(jnp.where(mine, here, 0), keys[past, columns], 1, 1) * scale
+            scores = jnp.where(causal, scores, -1e30)
+            highest = jnp.max(scores, axis=-1, keepdims=True)
+            powers = jnp.exp(scores - highest)
+            total = jnp.sum(powers, axis=-1, keepdims=True)
+            weights = (powers * (1.0 / total)).astype(jnp.bfloat16)
+            results.append(
+                jnp.dot(weights, values[past, columns], preferred_element_type=jnp.float32)
+            )
+            sums = jnp.where(lane == 2 * tile + head, highest + jnp.log(total), sums)
+        mixed[rows, columns] = jnp.where(lane < HD, results[0], results[1]).astype(jnp.bfloat16)
+        logsum[rows, :] = sums
+
+
+def turn_pairs(value, cosine, sine_low, sine_high, sign):
+    width = value.shape[1]
+    repeat = width // cosine.shape[1]
+    wide = lambda table: jnp.concatenate([table] * repeat, axis=1) if repeat > 1 else table
+    ahead = pltpu.roll(value, width - ROT // 2, 1)
+    behind = pltpu.roll(value, ROT // 2, 1)
+    return value * wide(cosine) + sign * (
+        ahead * wide(sine_low) + behind * wide(sine_high)
+    )
+
+
+def forward_kernel(
+    ways,
+    length,
+    block_input,
+    cotangent,
+    norm1_gain,
+    norm1_bias,
+    norm2_gain,
+    norm2_bias,
+    qkv_bias,
+    cosine,
+    sine_low,
+    sine_high,
+    qkv_hbm,
+    out_hbm,
+    gate_hbm,
+    up_hbm,
+    down_hbm,
+    rows_one,
+    query,
+    keys,
+    values,
+    logsum,
+    mixed,
+    attended,
+    rows_two,
+    grad_rows,
+    hidden,
+    grad_gate,
+    grad_up,
+    qkv_weight,
+    out_weight,
+    gate_weight,
+    up_weight,
+    down_weight,
+    grad_hidden,
+    held,
+    arrived,
+    load_sem,
+    gather_send,
+    gather_recv,
+    scatter_send,
+    scatter_recv,
+):
+    place = lax.axis_index("tensor")
+    loads = [
+        pltpu.make_async_copy(source, target, load_sem.at[i])
+        for i, (source, target) in enumerate(
+            (
+                (qkv_hbm, qkv_weight),
+                (out_hbm, out_weight),
+                (down_hbm, down_weight),
+                (gate_hbm, gate_weight),
+                (up_hbm, up_weight),
+            )
+        )
+    ]
+    for load in loads:
+        load.start()
+    line_barrier(place, ways)
+    size = block_input.shape[0]
+    own = pl.ds(pl.multiple_of(place * size, size), size)
+    one = LineGather(rows_one, place, ways, gather_send.at[0], gather_recv.at[0])
+    two = LineGather(rows_two, place, ways, gather_send.at[1], gather_recv.at[1])
+    back = LineGather(grad_rows, place, ways, gather_send.at[2], gather_recv.at[2])
+    rows_one[own, :] = norm_rows(
+        block_input[...].astype(jnp.float32), norm1_gain[...], norm1_bias[...]
+    ).astype(jnp.bfloat16)
+    one.start()
+    grad_rows[own, :] = cotangent[...]
+    loads[0].wait()
+
+    def project(slot):
+        rows = pl.ds(pl.multiple_of(slot * size, size), size)
+        spot = lax.rem(slot * size, length)
+        spots = pl.ds(pl.multiple_of(spot, size), size)
+        tables = cosine[spots, :], sine_low[spots, :], sine_high[spots, :]
+        for i, target in enumerate((query, keys, values)):
+            result = jnp.dot(
+                rows_one[rows, :], qkv_weight[i], preferred_element_type=jnp.float32
+            ) + qkv_bias[pl.ds(i, 1), :]
+            if i < 2:
+                result = turn_pairs(result, *tables, 1.0)
+            target[rows, :] = result.astype(jnp.bfloat16)
+
+    one.each(project)
+    back.start()
+    logsum[...] = jnp.zeros_like(logsum)
+    tiles = query.shape[1] // 128
+
+    def attend(i, carry):
+        base = pl.multiple_of((i // tiles) * length, length)
+        attention_tile(
+            length, query, keys, values, mixed, logsum, base, lax.rem(i, tiles)
+        )
+        return carry
+
+    lax.fori_loop(0, tiles * (rows_one.shape[0] // length), attend, 0)
+    one.drain()
+    loads[1].wait()
+    scatter = LineScatter(held, arrived, place, ways, scatter_send, scatter_recv)
+
+    def part(slot):
+        rows = pl.ds(pl.multiple_of(slot * size, size), size)
+        return jnp.dot(mixed[rows, :], out_weight[...], preferred_element_type=jnp.float32)
+
+    scatter.send_all(part, lambda i: back.hop(i + 1))
+    attended[...] = block_input[...].astype(jnp.float32) + part(place)
+    scatter.finish(attended)
+    rows_two[own, :] = norm_rows(attended[...], norm2_gain[...], norm2_bias[...]).astype(
+        jnp.bfloat16
+    )
+    two.start()
+    loads[2].wait()
+
+    def back_part(slot, carry):
+        rows = pl.ds(pl.multiple_of(slot * size, size), size)
+        grad_hidden[rows, :] = product(grad_rows[rows, :], down_weight[...], 1, 1)
+        return carry
+
+    lax.fori_loop(0, ways, back_part, 0)
+    loads[3].wait()
+    loads[4].wait()
+
+    def feed(slot):
+        rows = pl.ds(pl.multiple_of(slot * size, size), size)
+        gate = jnp.dot(rows_two[rows, :], gate_weight[...], preferred_element_type=jnp.float32)
+        upward = jnp.dot(rows_two[rows, :], up_weight[...], preferred_element_type=jnp.float32)
+        sigmoid = 1.0 / (1.0 + jnp.exp(-gate))
+        gated = gate * sigmoid
+        grad = grad_hidden[rows, :]
+        hidden[rows, :] = (gated * upward).astype(jnp.bfloat16)
+        grad_up[rows, :] = (grad * gated).astype(jnp.bfloat16)
+        grad_gate[rows, :] = (
+            grad * upward * sigmoid * (1.0 + gate * (1.0 - sigmoid))
+        ).astype(jnp.bfloat16)
+
+    two.each(feed)
+    two.drain()
+    back.drain()
+    scatter.drain()
+
+
+def rotary_lanes(length):
+    half_width = ROT // 2
+    frequency = rotary_base ** (-(jnp.arange(half_width, dtype=jnp.float32) * 2.0 / ROT))
+    angles = jnp.arange(length, dtype=jnp.float32)[:, None] * frequency[None, :]
+    cosine, sine = jnp.cos(angles), jnp.sin(angles)
+    zero = jnp.zeros((length, half_width), jnp.float32)
+    rest = jnp.zeros((length, HD - ROT), jnp.float32)
+    head = (
+        jnp.concatenate([cosine, cosine, rest + 1.0], axis=1),
+        jnp.concatenate([-sine, zero, rest], axis=1),
+        jnp.concatenate([zero, sine, rest], axis=1),
+    )
+    return [jnp.concatenate([table, table], axis=1) for table in head]
+
+
+def forward(ways, block_input, cotangent, norms, qkv_weight, qkv_bias, tables, weights):
+    size, width = block_input.shape
+    group = size * ways
+    inner = qkv_bias.shape[1]
+    out_weight, gate_weight, up_weight, down_weight = weights
+    units = gate_weight.shape[1]
+    low = lambda *shape: jax.ShapeDtypeStruct(shape, jnp.bfloat16)
+    full = lambda *shape: jax.ShapeDtypeStruct(shape, jnp.float32)
+    vmem = pl.BlockSpec(memory_space=pltpu.VMEM)
+    hbm = pl.BlockSpec(memory_space=pl.ANY)
+    shapes = (
+        low(group, width),
+        low(group, inner),
+        low(group, inner),
+        low(group, inner),
+        full(group, 128),
+        low(group, inner),
+        full(size, width),
+        low(group, width),
+        low(group, width),
+        low(group, units),
+        low(group, units),
+        low(group, units),
+    )
+    return pl.pallas_call(
+        functools.partial(forward_kernel, ways, LEN),
+        out_shape=shapes,
+        in_specs=[vmem] * 10 + [hbm] * 5,
+        out_specs=[vmem] * len(shapes),
+        scratch_shapes=[
+            pltpu.VMEM((3, width, inner), jnp.bfloat16),
+            pltpu.VMEM(out_weight.shape, jnp.bfloat16),
+            pltpu.VMEM(gate_weight.shape, jnp.bfloat16),
+            pltpu.VMEM(up_weight.shape, jnp.bfloat16),
+            pltpu.VMEM(down_weight.shape, jnp.bfloat16),
+            pltpu.VMEM((group, units), jnp.float32),
+            pltpu.VMEM((ways, size, width), jnp.bfloat16),
+            pltpu.VMEM((2, ways, size, width), jnp.bfloat16),
+            pltpu.SemaphoreType.DMA((5,)),
+            pltpu.SemaphoreType.DMA((3, 2, ways)),
+            pltpu.SemaphoreType.DMA((3, ways)),
+            pltpu.SemaphoreType.DMA((ways,)),
+            pltpu.SemaphoreType.DMA((2, ways)),
+        ],
+        compiler_params=pltpu.CompilerParams(
+            collective_id=0, has_side_effects=True, vmem_limit_bytes=67043328
+        ),
+    )(
+        block_input,
+        cotangent,
+        *norms,
+        qkv_bias,
+        *tables,
+        qkv_weight,
+        out_weight,
+        gate_weight,
+        up_weight,
+        down_weight,
+    )
+
+
 def body(
     ways,
+    tensor_ways,
     block_input,
     norm1_gain,
     norm1_bias,
@@ -152,45 +593,41 @@
     halver = Halver("dp", ways)
     cosine, sine_table = rotary_tables(LEN, ROT)
     stream = block_input.astype(jnp.float32)
-    normed, scaled_one, inverse_one = layer_norm(stream, norm1_gain, norm1_bias)
-    normed_one = normed.astype(jnp.bfloat16)
-    rows_one = lax.all_gather(normed_one, "tensor", axis=0, tiled=True)
+    (
+        rows_one,
+        query,
+        keys,
+        values,
+        logsum,
+        mixed,
+        attended,
+        rows_two,
+        grad_rows,
+        hidden,
+        grad_gate,
+        grad_up,
+    ) = forward(
+        tensor_ways,
+        block_input,
+        cotangent,
+        [row.reshape(1, width) for row in (norm1_gain, norm1_bias, norm2_gain, norm2_bias)],
+        jnp.transpose(qkv_weight, (1, 0, 2)),
+        qkv_bias,
+        rotary_lanes(LEN),
+        (out_weight, gate_weight, up_weight, down_weight),
+    )
     group = rows_one.shape[0]
     seq_count = group // LEN
-    projected = [
-        (jnp.dot(rows_one, part, preferred_element_type=jnp.float32) + bias).reshape(
-            seq_count, LEN, local_heads, HD
-        )
-        for part, bias in zip(parts, qkv_bias)
-    ]
-    query = rotate(projected[0], cosine, sine_table).astype(jnp.bfloat16)
-    keys = rotate(projected[1], cosine, sine_table).astype(jnp.bfloat16)
-    values = projected[2].astype(jnp.bfloat16)
-    scores = masked_scores(query, keys, scale)
-    highest = jnp.max(scores, axis=-1, keepdims=True)
-    logsum = highest + jnp.log(jnp.sum(jnp.exp(scores - highest), axis=-1, keepdims=True))
-    weights = jnp.exp(scores - logsum).astype(jnp.bfloat16)
-    mixed_heads = jnp.einsum(
-        "shqk,skhd->sqhd", weights, values, preferred_element_type=jnp.float32
-    ).astype(jnp.bfloat16)
-    mixed = mixed_heads.reshape(group, inner)
-    attended = stream + scatter_sum(jnp.dot(mixed, out_weight, preferred_element_type=jnp.float32))
-    normed, scaled_two, inverse_two = layer_norm(attended, norm2_gain, norm2_bias)
-    normed_two = normed.astype(jnp.bfloat16)
-    rows_two = lax.all_gather(normed_two, "tensor", axis=0, tiled=True)
-    gate = jnp.dot(rows_two, gate_weight, preferred_element_type=jnp.float32)
-    upward = jnp.dot(rows_two, up_weight, preferred_element_type=jnp.float32)
-    hidden = (jax.nn.silu(gate) * upward).astype(jnp.bfloat16)
+    query, keys, values, mixed_heads = (
+        piece.reshape(seq_count, LEN, local_heads, HD) for piece in (query, keys, values, mixed)
+    )
+    logsum = jnp.transpose(logsum[:, :local_heads].reshape(seq_count, LEN, local_heads), (0, 2, 1))
+    logsum = logsum[..., None]
+    _, scaled_one, inverse_one = layer_norm(stream, norm1_gain, norm1_bias)
+    _, scaled_two, inverse_two = layer_norm(attended, norm2_gain, norm2_bias)
     block_output = (
         attended + scatter_sum(jnp.dot(hidden, down_weight, preferred_element_type=jnp.float32))
     ).astype(jnp.bfloat16)
-    grad_rows = lax.all_gather(cotangent, "tensor", axis=0, tiled=True)
-    grad_hidden = product(grad_rows, down_weight, 1, 1)
-    gate_sigmoid = jax.nn.sigmoid(gate)
-    grad_gate = (grad_hidden * upward * gate_sigmoid * (1.0 + gate * (1.0 - gate_sigmoid))).astype(
-        jnp.bfloat16
-    )
-    grad_up = (grad_hidden * gate * gate_sigmoid).astype(jnp.bfloat16)
     grad_normed_two = scatter_sum(
         product(grad_gate, gate_weight, 1, 1) + product(grad_up, up_weight, 1, 1)
     )
@@ -299,4 +736,4 @@
         P(None, "tensor"),
         P("tensor", None),
     )
-    return jax.shard_map(functools.partial(body, mesh.shape["dp"]), mesh=mesh, in_specs=in_specs, out_specs=out_specs, check_vma=False)
+    return jax.shard_map(functools.partial(body, mesh.shape["dp"], mesh.shape["tensor"]), mesh=mesh, in_specs=in_specs, out_specs=out_specs, check_vma=False)

time: 674 us -> 589 us (0.87)
  waiting for transfers between devices: 294 us -> 110 us
  Pallas kernels: 0 us -> 130 us
  matrix products: 146 us -> 122 us
  other arithmetic: 73.4 us -> 59.6 us
    pallas_call x0 -> x1, Pallas kernels: none -> 130 us  [forward(): pl.pallas_call(functools.partial(forward_kernel, ways, LEN), out_shape=sh...]
    all_gather x3 -> x0, waiting for transfers between devices: 122 us -> none  [the longest x1 47.5 us: body(): rows_one = lax.all_gather(normed_one, 'tensor', axis=0, tiled=True)]
    reduce_scatter x4 -> x3, waiting for transfers between devices: 71.8 us -> 0.01 us  [scatter_sum(): lax.psum_scatter(value.astype(jnp.bfloat16), 'tensor', scatter_dimension=...]
    ppermute x42, waiting for transfers between devices: 73.1 us -> 110 us  [swap(): return lax.ppermute(value, self.axis, pairs)]
    dot_general x7 -> x0, matrix products: 31.7 us -> none  [the longest x3 10.6 us: body(): jnp.dot(rows_one, part, preferred_element_type=jnp.float32) + bias]
    all_gather x1, waiting for transfers between devices: 26.7 us -> 0.01 us  [body(): grad_attended = lax.all_gather(grad_low, 'tensor', axis=0, tiled=True)]
    another operation x13 -> x12, local copies, waits for them, and re-layouts: 11.8 us -> 15.5 us
    dot_general x35 -> x34, matrix products: 97 us -> 98.2 us  [product(): lax.dot_general(left, right, (((left_dim,), (right_dim,)), ((), ())), pre...]
  transfers between devices with their start and end apart: 50 -> 46, of which waited for: 25 -> 19; matrix products, arithmetic and copies ran while one was open for 30% -> 36% of each run, Pallas kernels for 0% -> 0%
where the time goes in v2:
time: 589 us; the launch traced here: 581 us
  Pallas kernels  130 us (22%)
  matrix products  122 us (21%)
  waiting for transfers between devices  110 us (19%)
  other arithmetic  59.6 us (10%)
  blocking collectives  54 us (9%)
  local copies, waits for them, and re-layouts  52.7 us (9%)
  starting transfers between devices  37.6 us (6%)
  between operations  15.5 us (3%)
    pallas_call x1, Pallas kernels, forward(): pl.pallas_call(functools.partial(forward_kernel, ways, LEN), out_shape=sh...  130 us
    ppermute x42, waiting for transfers between devices, swap(): return lax.ppermute(value, self.axis, pairs)  110 us
    dot_general x34, matrix products, product(): lax.dot_general(left, right, (((left_dim,), (right_dim,)), ((), ())), pre...  98.2 us
    psum x1, blocking collectives, body(): lax.psum((norm1_gain_part, norm1_bias_part, norm2_gain_part, norm2_bias_p...  37.9 us
    ppermute x42, starting transfers between devices, swap(): return lax.ppermute(value, self.axis, pairs)  36.7 us
    dynamic_update_slice x14, other arithmetic, spread(): lax.dynamic_update_slice_in_dim(whole, piece.astype(kind), keep * size, 0)  25.8 us
    psum x1, blocking collectives, body(): bias_grad = lax.psum(bias_grad, 'dp')  16.2 us
    another operation x12, local copies, waits for them, and re-layouts  15.5 us
  transfers between devices with their start and end apart: 46, of which 19 were waited for; matrix products, arithmetic and copies ran while one was open for 36% of the time, Pallas kernels for 0%

profile of v2, /device:TPU:0, one launch (start us, length us, event | category | flops | bytes accessed | tf_op | source)
XLA Modules:
  0.0 581.4 jit_solution(7991286572933661047)
XLA Ops:
  11.7 130.3 %shard_map.211 = (bf16[512,2048]{1,0:T(8,128)(2,1)}, bf16[512,512]{1,0:T(8,128)(2,1)}, bf16[512,512]{1,0:T(8,128)(2,1)}, bf16[512,512]{1,0:T(8,128)(2,1)}, f32[5...) custom-call(bf16[128,2048]{1,0:T(8,128)(2,1)} %block_input.1, ...), custom_call_target="tpu_custom_call" | custom-call | tf_op jit(solution)/shard_map/pallas_call | solution.py:535
  142.0 6.0 %fusion.155 = f32[512,2048]{1,0:T(8,128)S(1)} fusion(bf16[512,1408]{1,0:T(8,128)(2,1)} %get-tuple-element.26, bf16[2048,1408]{1,0:T(8,128)(2,1)} %gate_hbm.1), kind=kOutput, calls=%fused_computation.237 | convolution fusion | flops 2952790016 | bytes 11403264 | tf_op jit(solution)/shard_map/dot_general | solution.py:60
  148.0 7.3 %add_convert_fusion.1 = bf16[512,2048]{1,0:T(8,128)(2,1)} fusion(f32[512,2048]{1,0:T(8,128)S(1)} %fusion.155, bf16[512,1408]{1,0:T(8,128)(2,1)S(1)} %copy-done.18, bf16[2048,1408]{1,0:T(8,128)(2,1)} %up_hbm.1), kind=kOutput, calls=%fused_computation.11 | convolution fusion | flops 2954887168 | bytes 13500416 | tf_op jit(solution)/shard_map/dot_general | solution.py:60
  156.9 4.6 convolution_convert_fusion.2
  161.5 4.8 convolution_convert_fusion
  166.8 3.4 convolution_convert_fusion.1
  170.3 7.4 %convolution_convert_fusion.3 = bf16[512,2048]{1,0:T(8,128)(2,1)} fusion(bf16[512,1408]{1,0:T(8,128)(2,1)S(1)} %copy-done.38, bf16[1408,2048]{1,0:T(8,128)(2,1)} %down_hbm.1), kind=kOutput, calls=%fused_computation.17 | convolution fusion | flops 2953838592 | bytes 9306112 | tf_op jit(solution)/shard_map/dot_general | solution.py:629
  181.3 2.7 fusion.87
  186.6 2.8 fusion.74
  189.4 3.7 add_convert_fusion.2
  200.1 4.2 add_convert_fusion.3
  204.8 3.8 add_convert_fusion.4
  210.2 4.7 fusion.156
  214.9 3.1 add_convert_fusion.6
  223.9 11.1 %collective-permute-done.31 = bf16[512,1408]{1,0:T(8,128)(2,1)} collective-permute-done((bf16[512,1408]{1,0:T(8,128)(2,1)}, bf16[512,1408]{1,0:T(8,128)(2,1)}, u32[]{:S(2)}, u32[]{:S(2)}) %collective-permute-start.31) | collective-permute-done | bytes 1441824 | tf_op jit(solution)/shard_map/ppermute | solution.py:94
  239.6 19.1 %collective-permute-done.25 = bf16[512,1408]{1,0:T(8,128)(2,1)} collective-permute-done((bf16[512,1408]{1,0:T(8,128)(2,1)}, bf16[512,1408]{1,0:T(8,128)(2,1)}, u32[]{:S(2)}, u32[]{:S(2)}) %collective-permute-start.25) | collective-permute-done | bytes 1441824 | tf_op jit(solution)/shard_map/ppermute | solution.py:94
  262.5 3.1 constant_dynamic-update-slice_fusion.13
  267.4 2.9 constant_dynamic-update-slice_fusion.3
  273.3 2.8 constant_dynamic-update-slice_fusion.7
  282.7 9.9 %collective-permute-done.33 = bf16[256,1408]{1,0:T(8,128)(2,1)} collective-permute-done((bf16[256,1408]{1,0:T(8,128)(2,1)}, bf16[256,1408]{1,0:T(8,128)(2,1)}, u32[]{:S(2)}, u32[]{:S(2)}) %collective-permute-start.33) | collective-permute-done | bytes 720928 | tf_op jit(solution)/shard_map/ppermute | solution.py:94
  296.3 11.8 %collective-permute-done.27 = bf16[256,1408]{1,0:T(8,128)(2,1)} collective-permute-done((bf16[256,1408]{1,0:T(8,128)(2,1)}, bf16[256,1408]{1,0:T(8,128)(2,1)}, u32[]{:S(2)}, u32[]{:S(2)}) %collective-permute-start.27) | collective-permute-done | bytes 720928 | tf_op jit(solution)/shard_map/ppermute | solution.py:94
  311.6 3.2 fusion.150
  321.7 3.3 collective-permute-done.34
  330.6 9.8 %collective-permute-done.28 = bf16[512,1408]{1,0:T(8,128)(2,1)} collective-permute-done((bf16[512,1408]{1,0:T(8,128)(2,1)}, bf16[512,1408]{1,0:T(8,128)(2,1)}, u32[]{:S(2)}, u32[]{:S(2)}) %collective-permute-start.28) | collective-permute-done | bytes 1441824 | tf_op jit(solution)/shard_map/ppermute | solution.py:94
  344.2 5.6 broadcast.129.clone.1
  349.7 6.7 %convert_dynamic-update-slice_fusion.3 = f32[2048,1408]{1,0:T(8,128)} fusion(f32[2048,1408]{1,0:T(8,128)} %broadcast.129.clone.1, s32[]{:T(128)S(6)} %select_n.227, bf16[1024,1408]{1,0:T(8,128)(2,1)} %constant_dynamic-update-slice_fusion), kind=kLoop, calls=%fused_computation.7 | loop fusion | flops 1441792 | bytes 8650756 | tf_op jit(solution)/shard_map/dynamic_update_slice | solution.py:123
  356.4 5.2 broadcast.129.clone
  361.6 2.9 convert_dynamic-update-slice_fusion.5
  364.5 3.0 fusion.35
  367.6 5.7 multiply_convert_fusion
  375.8 3.4 fusion.152
  380.1 3.3 fusion.5
  386.9 3.3 fusion.7
  394.0 3.2 convolution_convert_fusion.5
  397.3 6.8 %add_convert_fusion = bf16[512,2048]{1,0:T(8,128)(2,1)} fusion(f32[512,2048]{1,0:T(8,128)} %fusion.7, f32[512,2048]{1,0:T(8,128)} %fusion.5, bf16[512,512]{0,1:T(8,128)(2,1)S(1)} %bitcast.130, bf16[2048,3,512]{2,0,1:T(8,128)(2,1)} %param.15), kind=kOutput, calls=%fused_computation.10 | convolution fusion | flops 1076887552 | bytes 13107200 | tf_op jit(solution)/shard_map/dot_general | solution.py:60
  410.7 16.2 %psum.37 = f32[3,512]{1,0:T(4,128)} all-reduce(f32[3,512]{1,0:T(4,128)S(1)} %pad_maximum_fusion.5), channel_id=1, replica_groups=mesh['dp'=8,'tensor'=4] {'dp'}, use_global_device_ids=true, to_apply=%region_18.19 | all-reduce | flops 1536 | bytes 12288 | tf_op jit(solution)/shard_map/psum | solution.py:689
  441.1 4.0 collective-permute-done.1
  446.9 6.6 %collective-permute-done.7 = bf16[512,512]{1,0:T(8,128)(2,1)S(1)} collective-permute-done((bf16[512,512]{1,0:T(8,128)(2,1)S(1)}, bf16[512,512]{1,0:T(8,128)(2,1)S(1)}, u32[]{:S(2)}, u32[]{:S(2)}) %collective-permute-start.7) | collective-permute-done | bytes 524320 | tf_op jit(solution)/shard_map/ppermute | solution.py:94
  455.3 6.6 %collective-permute-done.13 = bf16[512,512]{1,0:T(8,128)(2,1)S(1)} collective-permute-done((bf16[512,512]{1,0:T(8,128)(2,1)S(1)}, bf16[512,512]{1,0:T(8,128)(2,1)S(1)}, u32[]{:S(2)}, u32[]{:S(2)}) %collective-permute-start.13) | collective-permute-done | bytes 524320 | tf_op jit(solution)/shard_map/ppermute | solution.py:94
  472.9 3.9 collective-permute-done.3
  477.8 4.2 collective-permute-done.9
  482.2 5.5 collective-permute-done.15
  493.7 4.1 collective-permute-done.10
  499.4 4.1 collective-permute-done.16
  511.3 5.2 convert_dynamic-update-slice_fusion.2
  517.2 2.9 convert_dynamic-update-slice_fusion.4
  527.4 5.2 pad_maximum_fusion
  534.1 37.9 %all-reduce = (f32[2048]{0:T(1024)}, f32[2048]{0:T(1024)}, f32[2048]{0:T(1024)}, f32[2048]{0:T(1024)}) all-reduce(f32[2048]{0:T(1024)S(1)} %get-tuple-element.38, f32[2048]{0:T(1024)S(1)} %get-tuple-element.43, f32[2048]{0:T(1024)S(1)} %get-tuple-element.36, ...), channel_id=1, replica_groups=mesh['dp'=8,'tensor'=4] {'dp','tensor'}, use_global_device_ids=true, to_apply=%region_12.13 | all-reduce | flops 8192 | bytes 65536 | tf_op jit(solution)/shard_map/psum | solution.py:686
  (310 shorter events, 145.0 us)
Async XLA Ops:
  7.2 270.5 %reduce-scatter.6.cloned.1.call-start = ((), (), s32[]{:S(2)}) async-start(), calls=%async_computation.4 | async-start | bytes 2621440 | tf_op jit(solution)/shard_map/reduce_scatter | solution.py:129
  155.3 156.3 %reduce-scatter.4.cloned.1.call-start = ((), (), s32[]{:S(2)}) async-start(), calls=%async_computation.3 | async-start | bytes 2621440 | tf_op jit(solution)/shard_map/reduce_scatter | solution.py:129
  161.5 27.9 %collective-permute-start.36 = (bf16[704,2048]{1,0:T(8,128)(2,1)}, bf16[704,2048]{1,0:T(8,128)(2,1)}, u32[]{:S(2)}, u32[]{:S(2)}) collective-permute-start(bf16[704,2048]{1,0:T(8,128)(2,1)} %convolution_convert_fusion.2), channel_id=1, source_target_pairs={{0,4},{4,0},{8,12},{12,8},{16,20},{20,16},{24,28},{28,24},{1,5},{5... | collective-permute-start | bytes 8650760 | tf_op jit(solution)/shard_map/ppermute | solution.py:94
  166.3 33.8 %collective-permute-start.30 = (bf16[1024,1408]{1,0:T(8,128)(2,1)}, bf16[1024,1408]{1,0:T(8,128)(2,1)}, u32[]{:S(2)}, u32[]{:S(2)}) collective-permute-start(bf16[1024,1408]{1,0:T(8,128)(2,1)} %convolution_convert_fusion), channel_id=1, source_target_pairs={{0,4},{4,0},{8,12},{12,8},{16,20},{20,16},{24,28},{28,24},{1,5},{5... | collective-permute-start | bytes 8650760 | tf_op jit(solution)/shard_map/ppermute | solution.py:94
  170.2 34.6 %collective-permute-start.24 = (bf16[1024,1408]{1,0:T(8,128)(2,1)}, bf16[1024,1408]{1,0:T(8,128)(2,1)}, u32[]{:S(2)}, u32[]{:S(2)}) collective-permute-start(bf16[1024,1408]{1,0:T(8,128)(2,1)} %convolution_convert_fusion.1), channel_id=1, source_target_pairs={{0,4},{4,0},{8,12},{12,8},{16,20},{20,16},{24,28},{28,24},{1,5},{5... | collective-permute-start | bytes 8650760 | tf_op jit(solution)/shard_map/ppermute | solution.py:94
  177.7 186.8 %all-gather.2.cloned.1.call-start = ((), (), s32[]{:S(2)}) async-start(), calls=%async_computation.5 | async-start | bytes 2621440 | tf_op jit(solution)/shard_map/all_gather | solution.py:643
  193.1 21.9 %collective-permute-start.37 = (bf16[352,2048]{1,0:T(8,128)(2,1)}, bf16[352,2048]{1,0:T(8,128)(2,1)}, u32[]{:S(2)}, u32[]{:S(2)}) collective-permute-start(bf16[352,2048]{1,0:T(8,128)(2,1)} %add_convert_fusion.2), channel_id=1, source_target_pairs={{0,8},{4,20},{8,0},{12,28},{16,24},{20,4},{24,16},{28,12},{1,9},{5... | collective-permute-start | bytes 4325384 | tf_op jit(solution)/shard_map/ppermute | solution.py:94
  204.3 30.7 %collective-permute-start.31 = (bf16[512,1408]{1,0:T(8,128)(2,1)}, bf16[512,1408]{1,0:T(8,128)(2,1)}, u32[]{:S(2)}, u32[]{:S(2)}) collective-permute-start(bf16[512,1408]{1,0:T(8,128)(2,1)} %add_convert_fusion.3), channel_id=1, source_target_pairs={{0,8},{4,20},{8,0},{12,28},{16,24},{20,4},{24,16},{28,12},{1,9},{5... | collective-permute-start | bytes 4325384 | tf_op jit(solution)/shard_map/ppermute | solution.py:94
  208.6 50.1 %collective-permute-start.25 = (bf16[512,1408]{1,0:T(8,128)(2,1)}, bf16[512,1408]{1,0:T(8,128)(2,1)}, u32[]{:S(2)}, u32[]{:S(2)}) collective-permute-start(bf16[512,1408]{1,0:T(8,128)(2,1)} %add_convert_fusion.4), channel_id=1, source_target_pairs={{0,8},{4,20},{8,0},{12,28},{16,24},{20,4},{24,16},{28,12},{1,9},{5... | collective-permute-start | bytes 4325384 | tf_op jit(solution)/shard_map/ppermute | solution.py:94
  218.0 44.4 %collective-permute-start.38 = (bf16[176,2048]{1,0:T(8,128)(2,1)}, bf16[176,2048]{1,0:T(8,128)(2,1)}, u32[]{:S(2)}, u32[]{:S(2)}) collective-permute-start(bf16[176,2048]{1,0:T(8,128)(2,1)} %add_convert_fusion.6), channel_id=1, source_target_pairs={{0,16},{4,12},{8,24},{12,4},{16,0},{20,28},{24,8},{28,20},{1,17},{... | collective-permute-start | bytes 2162696 | tf_op jit(solution)/shard_map/ppermute | solution.py:94
  223.8 34.9 %copy-start.17 = (bf16[512,1408]{1,0:T(8,128)(2,1)S(1)}, bf16[512,1408]{1,0:T(8,128)(2,1)}, u32[]{:S(2)}) copy-start(bf16[512,1408]{1,0:T(8,128)(2,1)} %get-tuple-element.26) | copy-start | bytes 4325380
  237.5 28.7 %collective-permute-start.32 = (bf16[256,1408]{1,0:T(8,128)(2,1)S(1)}, bf16[256,1408]{1,0:T(8,128)(2,1)S(1)}, u32[]{:S(2)}, u32[]{:S(2)}) collective-permute-start(bf16[256,1408]{1,0:T(8,128)(2,1)S(1)} %add_convert_fusion.8), channel_id=1, source_target_pairs={{0,16},{4,12},{8,24},{12,4},{16,0},{20,28},{24,8},{28,20},{1,17},{... | collective-permute-start | bytes 2162696 | tf_op jit(solution)/shard_map/ppermute | solution.py:94
  260.8 11.4 %collective-permute-start.26 = (bf16[256,1408]{1,0:T(8,128)(2,1)S(1)}, bf16[256,1408]{1,0:T(8,128)(2,1)S(1)}, u32[]{:S(2)}, u32[]{:S(2)}) collective-permute-start(bf16[256,1408]{1,0:T(8,128)(2,1)S(1)} %add_convert_fusion.10), channel_id=1, source_target_pairs={{0,16},{4,12},{8,24},{12,4},{16,0},{20,28},{24,8},{28,20},{1,17},{... | collective-permute-start | bytes 2162696 | tf_op jit(solution)/shard_map/ppermute | solution.py:94
  265.6 14.3 %collective-permute-start.39 = (bf16[176,2048]{1,0:T(8,128)(2,1)}, bf16[176,2048]{1,0:T(8,128)(2,1)}, u32[]{:S(2)}, u32[]{:S(2)}) collective-permute-start(bf16[176,2048]{1,0:T(8,128)(2,1)} %get-tuple-element.49), channel_id=1, source_target_pairs={{0,16},{4,12},{8,24},{12,4},{16,0},{20,28},{24,8},{28,20},{1,17},{... | collective-permute-start | bytes 2162696 | tf_op jit(solution)/shard_map/ppermute | solution.py:94
  270.2 22.4 %collective-permute-start.33 = (bf16[256,1408]{1,0:T(8,128)(2,1)}, bf16[256,1408]{1,0:T(8,128)(2,1)}, u32[]{:S(2)}, u32[]{:S(2)}) collective-permute-start(bf16[256,1408]{1,0:T(8,128)(2,1)} %get-tuple-element.51), channel_id=1, source_target_pairs={{0,16},{4,12},{8,24},{12,4},{16,0},{20,28},{24,8},{28,20},{1,17},{... | collective-permute-start | bytes 2162696 | tf_op jit(solution)/shard_map/ppermute | solution.py:94
  276.1 32.0 %collective-permute-start.27 = (bf16[256,1408]{1,0:T(8,128)(2,1)}, bf16[256,1408]{1,0:T(8,128)(2,1)}, u32[]{:S(2)}, u32[]{:S(2)}) collective-permute-start(bf16[256,1408]{1,0:T(8,128)(2,1)} %get-tuple-element.53), channel_id=1, source_target_pairs={{0,16},{4,12},{8,24},{12,4},{16,0},{20,28},{24,8},{28,20},{1,17},{... | collective-permute-start | bytes 2162696 | tf_op jit(solution)/shard_map/ppermute | solution.py:94
  281.2 47.8 %collective-permute-start.40 = (bf16[352,2048]{1,0:T(8,128)(2,1)S(1)}, bf16[352,2048]{1,0:T(8,128)(2,1)}, u32[]{:S(2)}, u32[]{:S(2)}) collective-permute-start(bf16[352,2048]{1,0:T(8,128)(2,1)S(1)} %constant_dynamic-update-slice_fusion.22), channel_id=1, source_target_pairs={{0,8},{4,20},{8,0},{12,28},{16,24},{20,4},{24,16},{28,12},{1,9},{5... | collective-permute-start | bytes 4325384 | tf_op jit(solution)/shard_map/ppermute | solution.py:94
  294.6 30.3 %collective-permute-start.34 = (bf16[512,1408]{1,0:T(8,128)(2,1)}, bf16[512,1408]{1,0:T(8,128)(2,1)}, u32[]{:S(2)}, u32[]{:S(2)}) collective-permute-start(bf16[512,1408]{1,0:T(8,128)(2,1)} %constant_dynamic-update-slice_fusion.2), channel_id=1, source_target_pairs={{0,8},{4,20},{8,0},{12,28},{16,24},{20,4},{24,16},{28,12},{1,9},{5... | collective-permute-start | bytes 4325384 | tf_op jit(solution)/shard_map/ppermute | solution.py:94
  310.1 30.3 %collective-permute-start.28 = (bf16[512,1408]{1,0:T(8,128)(2,1)}, bf16[512,1408]{1,0:T(8,128)(2,1)}, u32[]{:S(2)}, u32[]{:S(2)}) collective-permute-start(bf16[512,1408]{1,0:T(8,128)(2,1)} %constant_dynamic-update-slice_fusion.6), channel_id=1, source_target_pairs={{0,8},{4,20},{8,0},{12,28},{16,24},{20,4},{24,16},{28,12},{1,9},{5... | collective-permute-start | bytes 4325384 | tf_op jit(solution)/shard_map/ppermute | solution.py:94
  314.8 217.8 %reduce-scatter.8.cloned.1.call-start = ((), (), s32[]{:S(2)}) async-start(), calls=%async_computation.6 | async-start | bytes 2621440 | tf_op jit(solution)/shard_map/reduce_scatter | solution.py:129
  327.6 183.7 %collective-permute-start.35 = (bf16[1024,1408]{1,0:T(8,128)(2,1)}, bf16[1024,1408]{1,0:T(8,128)(2,1)}, u32[]{:S(2)}, u32[]{:S(2)}) collective-permute-start(bf16[1024,1408]{1,0:T(8,128)(2,1)} %constant_dynamic-update-slice_fusion), channel_id=1, source_target_pairs={{0,4},{4,0},{8,12},{12,8},{16,20},{20,16},{24,28},{28,24},{1,5},{5... | collective-permute-start | bytes 8650760 | tf_op jit(solution)/shard_map/ppermute | solution.py:94
  391.9 36.6 %collective-permute-start.18 = (bf16[256,2048]{1,0:T(8,128)(2,1)}, bf16[256,2048]{1,0:T(8,128)(2,1)}, u32[]{:S(2)}, u32[]{:S(2)}) collective-permute-start(bf16[256,2048]{1,0:T(8,128)(2,1)} %convolution_convert_fusion.4), channel_id=1, source_target_pairs={{0,4},{4,0},{8,12},{12,8},{16,20},{20,16},{24,28},{28,24},{1,5},{5... | collective-permute-start | bytes 3145736 | tf_op jit(solution)/shard_map/ppermute | solution.py:94
  393.5 36.7 %collective-permute-start = (bf16[1024,512]{1,0:T(8,128)(2,1)}, bf16[1024,512]{1,0:T(8,128)(2,1)}, u32[]{:S(2)}, u32[]{:S(2)}) collective-permute-start(bf16[1024,512]{1,0:T(8,128)(2,1)} %convolution_convert_fusion.7), channel_id=1, source_target_pairs={{0,4},{4,0},{8,12},{12,8},{16,20},{20,16},{24,28},{28,24},{1,5},{5... | collective-permute-start | bytes 3145736 | tf_op jit(solution)/shard_map/ppermute | solution.py:94
  393.5 38.3 %collective-permute-start.6 = (bf16[1024,512]{1,0:T(8,128)(2,1)}, bf16[1024,512]{1,0:T(8,128)(2,1)}, u32[]{:S(2)}, u32[]{:S(2)}) collective-permute-start(bf16[1024,512]{1,0:T(8,128)(2,1)} %convolution_convert_fusion.6), channel_id=1, source_target_pairs={{0,4},{4,0},{8,12},{12,8},{16,20},{20,16},{24,28},{28,24},{1,5},{5... | collective-permute-start | bytes 3145736 | tf_op jit(solution)/shard_map/ppermute | solution.py:94
  397.2 38.2 %collective-permute-start.12 = (bf16[1024,512]{1,0:T(8,128)(2,1)}, bf16[1024,512]{1,0:T(8,128)(2,1)}, u32[]{:S(2)}, u32[]{:S(2)}) collective-permute-start(bf16[1024,512]{1,0:T(8,128)(2,1)} %convolution_convert_fusion.5), channel_id=1, source_target_pairs={{0,4},{4,0},{8,12},{12,8},{16,20},{20,16},{24,28},{28,24},{1,5},{5... | collective-permute-start | bytes 3145736 | tf_op jit(solution)/shard_map/ppermute | solution.py:94
  428.5 88.0 %collective-permute-start.29 = (bf16[1024,1408]{1,0:T(8,128)(2,1)}, bf16[1024,1408]{1,0:T(8,128)(2,1)S(1)}, u32[]{:S(2)}, u32[]{:S(2)}) collective-permute-start(bf16[1024,1408]{1,0:T(8,128)(2,1)} %copy-done.8), channel_id=1, source_target_pairs={{0,4},{4,0},{8,12},{12,8},{16,20},{20,16},{24,28},{28,24},{1,5},{5... | collective-permute-start | bytes 8650760 | tf_op jit(solution)/shard_map/ppermute | solution.py:94
  430.2 9.2 %collective-permute-start.19 = (bf16[128,2048]{1,0:T(8,128)(2,1)S(1)}, bf16[128,2048]{1,0:T(8,128)(2,1)S(1)}, u32[]{:S(2)}, u32[]{:S(2)}) collective-permute-start(bf16[128,2048]{1,0:T(8,128)(2,1)S(1)} %add_convert_fusion.11), channel_id=1, source_target_pairs={{0,8},{4,20},{8,0},{12,28},{16,24},{20,4},{24,16},{28,12},{1,9},{5... | collective-permute-start | bytes 1572872 | tf_op jit(solution)/shard_map/ppermute | solution.py:94
  431.9 13.2 %collective-permute-start.1 = (bf16[512,512]{1,0:T(8,128)(2,1)S(1)}, bf16[512,512]{1,0:T(8,128)(2,1)S(1)}, u32[]{:S(2)}, u32[]{:S(2)}) collective-permute-start(bf16[512,512]{1,0:T(8,128)(2,1)S(1)} %add_convert_fusion.14), channel_id=1, source_target_pairs={{0,8},{4,20},{8,0},{12,28},{16,24},{20,4},{24,16},{28,12},{1,9},{5... | collective-permute-start | bytes 1572872 | tf_op jit(solution)/shard_map/ppermute | solution.py:94
  435.5 18.0 %collective-permute-start.7 = (bf16[512,512]{1,0:T(8,128)(2,1)S(1)}, bf16[512,512]{1,0:T(8,128)(2,1)S(1)}, u32[]{:S(2)}, u32[]{:S(2)}) collective-permute-start(bf16[512,512]{1,0:T(8,128)(2,1)S(1)} %add_convert_fusion.13), channel_id=1, source_target_pairs={{0,8},{4,20},{8,0},{12,28},{16,24},{20,4},{24,16},{28,12},{1,9},{5... | collective-permute-start | bytes 1572872 | tf_op jit(solution)/shard_map/ppermute | solution.py:94
  439.5 22.5 %collective-permute-start.13 = (bf16[512,512]{1,0:T(8,128)(2,1)S(1)}, bf16[512,512]{1,0:T(8,128)(2,1)S(1)}, u32[]{:S(2)}, u32[]{:S(2)}) collective-permute-start(bf16[512,512]{1,0:T(8,128)(2,1)S(1)} %add_convert_fusion.12), channel_id=1, source_target_pairs={{0,8},{4,20},{8,0},{12,28},{16,24},{20,4},{24,16},{28,12},{1,9},{5... | collective-permute-start | bytes 1572872 | tf_op jit(solution)/shard_map/ppermute | solution.py:94
  445.1 18.6 %collective-permute-start.20 = (bf16[64,2048]{1,0:T(8,128)(2,1)S(1)}, bf16[64,2048]{1,0:T(8,128)(2,1)S(1)}, u32[]{:S(2)}, u32[]{:S(2)}) collective-permute-start(bf16[64,2048]{1,0:T(8,128)(2,1)S(1)} %add_convert_fusion.17), channel_id=1, source_target_pairs={{0,16},{4,12},{8,24},{12,4},{16,0},{20,28},{24,8},{28,20},{1,17},{... | collective-permute-start | bytes 786440 | tf_op jit(solution)/shard_map/ppermute | solution.py:94
  453.5 13.1 %collective-permute-start.2 = (bf16[256,512]{1,0:T(8,128)(2,1)S(1)}, bf16[256,512]{1,0:T(8,128)(2,1)S(1)}, u32[]{:S(2)}, u32[]{:S(2)}) collective-permute-start(bf16[256,512]{1,0:T(8,128)(2,1)S(1)} %add_convert_fusion.23), channel_id=1, source_target_pairs={{0,16},{4,12},{8,24},{12,4},{16,0},{20,28},{24,8},{28,20},{1,17},{... | collective-permute-start | bytes 786440 | tf_op jit(solution)/shard_map/ppermute | solution.py:94
  461.9 6.4 %collective-permute-start.8 = (bf16[256,512]{1,0:T(8,128)(2,1)S(1)}, bf16[256,512]{1,0:T(8,128)(2,1)S(1)}, u32[]{:S(2)}, u32[]{:S(2)}) collective-permute-start(bf16[256,512]{1,0:T(8,128)(2,1)S(1)} %add_convert_fusion.21), channel_id=1, source_target_pairs={{0,16},{4,12},{8,24},{12,4},{16,0},{20,28},{24,8},{28,20},{1,17},{... | collective-permute-start | bytes 786440 | tf_op jit(solution)/shard_map/ppermute | solution.py:94
  463.7 7.4 %collective-permute-start.14 = (bf16[256,512]{1,0:T(8,128)(2,1)S(1)}, bf16[256,512]{1,0:T(8,128)(2,1)S(1)}, u32[]{:S(2)}, u32[]{:S(2)}) collective-permute-start(bf16[256,512]{1,0:T(8,128)(2,1)S(1)} %add_convert_fusion.19), channel_id=1, source_target_pairs={{0,16},{4,12},{8,24},{12,4},{16,0},{20,28},{24,8},{28,20},{1,17},{... | collective-permute-start | bytes 786440 | tf_op jit(solution)/shard_map/ppermute | solution.py:94
  466.6 10.8 %collective-permute-start.21 = (bf16[64,2048]{1,0:T(8,128)(2,1)S(1)}, bf16[64,2048]{1,0:T(8,128)(2,1)S(1)}, u32[]{:S(2)}, u32[]{:S(2)}) collective-permute-start(bf16[64,2048]{1,0:T(8,128)(2,1)S(1)} %get-tuple-element.55), channel_id=1, source_target_pairs={{0,16},{4,12},{8,24},{12,4},{16,0},{20,28},{24,8},{28,20},{1,17},{... | collective-permute-start | bytes 786440 | tf_op jit(solution)/shard_map/ppermute | solution.py:94
  468.3 8.4 %collective-permute-start.3 = (bf16[256,512]{1,0:T(8,128)(2,1)S(1)}, bf16[256,512]{1,0:T(8,128)(2,1)S(1)}, u32[]{:S(2)}, u32[]{:S(2)}) collective-permute-start(bf16[256,512]{1,0:T(8,128)(2,1)S(1)} %get-tuple-element.57), channel_id=1, source_target_pairs={{0,16},{4,12},{8,24},{12,4},{16,0},{20,28},{24,8},{28,20},{1,17},{... | collective-permute-start | bytes 786440 | tf_op jit(solution)/shard_map/ppermute | solution.py:94
  471.1 10.9 %collective-permute-start.9 = (bf16[256,512]{1,0:T(8,128)(2,1)S(1)}, bf16[256,512]{1,0:T(8,128)(2,1)S(1)}, u32[]{:S(2)}, u32[]{:S(2)}) collective-permute-start(bf16[256,512]{1,0:T(8,128)(2,1)S(1)} %get-tuple-element.59), channel_id=1, source_target_pairs={{0,16},{4,12},{8,24},{12,4},{16,0},{20,28},{24,8},{28,20},{1,17},{... | collective-permute-start | bytes 786440 | tf_op jit(solution)/shard_map/ppermute | solution.py:94
  476.7 10.9 %collective-permute-start.15 = (bf16[256,512]{1,0:T(8,128)(2,1)S(1)}, bf16[256,512]{1,0:T(8,128)(2,1)S(1)}, u32[]{:S(2)}, u32[]{:S(2)}) collective-permute-start(bf16[256,512]{1,0:T(8,128)(2,1)S(1)} %get-tuple-element.61), channel_id=1, source_target_pairs={{0,16},{4,12},{8,24},{12,4},{16,0},{20,28},{24,8},{28,20},{1,17},{... | collective-permute-start | bytes 786440 | tf_op jit(solution)/shard_map/ppermute | solution.py:94
  477.4 10.3 %collective-permute-start.4 = (bf16[512,512]{1,0:T(8,128)(2,1)S(1)}, bf16[512,512]{1,0:T(8,128)(2,1)S(1)}, u32[]{:S(2)}, u32[]{:S(2)}) collective-permute-start(bf16[512,512]{1,0:T(8,128)(2,1)S(1)} %constant_dynamic-update-slice_fusion.25), channel_id=1, source_target_pairs={{0,8},{4,20},{8,0},{12,28},{16,24},{20,4},{24,16},{28,12},{1,9},{5... | collective-permute-start | bytes 1572872 | tf_op jit(solution)/shard_map/ppermute | solution.py:94
  482.0 10.2 %collective-permute-start.22 = (bf16[128,2048]{1,0:T(8,128)(2,1)S(1)}, bf16[128,2048]{1,0:T(8,128)(2,1)S(1)}, u32[]{:S(2)}, u32[]{:S(2)}) collective-permute-start(bf16[128,2048]{1,0:T(8,128)(2,1)S(1)} %constant_dynamic-update-slice_fusion.11), channel_id=1, source_target_pairs={{0,8},{4,20},{8,0},{12,28},{16,24},{20,4},{24,16},{28,12},{1,9},{5... | collective-permute-start | bytes 1572872 | tf_op jit(solution)/shard_map/ppermute | solution.py:94
  487.6 10.2 %collective-permute-start.10 = (bf16[512,512]{1,0:T(8,128)(2,1)S(1)}, bf16[512,512]{1,0:T(8,128)(2,1)S(1)}, u32[]{:S(2)}, u32[]{:S(2)}) collective-permute-start(bf16[512,512]{1,0:T(8,128)(2,1)S(1)} %constant_dynamic-update-slice_fusion.20), channel_id=1, source_target_pairs={{0,8},{4,20},{8,0},{12,28},{16,24},{20,4},{24,16},{28,12},{1,9},{5... | collective-permute-start | bytes 1572872 | tf_op jit(solution)/shard_map/ppermute | solution.py:94
  487.7 15.8 %collective-permute-start.16 = (bf16[512,512]{1,0:T(8,128)(2,1)S(1)}, bf16[512,512]{1,0:T(8,128)(2,1)S(1)}, u32[]{:S(2)}, u32[]{:S(2)}) collective-permute-start(bf16[512,512]{1,0:T(8,128)(2,1)S(1)} %constant_dynamic-update-slice_fusion.16), channel_id=1, source_target_pairs={{0,8},{4,20},{8,0},{12,28},{16,24},{20,4},{24,16},{28,12},{1,9},{5... | collective-permute-start | bytes 1572872 | tf_op jit(solution)/shard_map/ppermute | solution.py:94
  492.2 27.9 %collective-permute-start.41 = (bf16[704,2048]{1,0:T(8,128)(2,1)S(1)}, bf16[704,2048]{1,0:T(8,128)(2,1)S(1)}, u32[]{:S(2)}, u32[]{:S(2)}) collective-permute-start(bf16[704,2048]{1,0:T(8,128)(2,1)S(1)} %copy-done.7), channel_id=1, source_target_pairs={{0,4},{4,0},{8,12},{12,8},{16,20},{20,16},{24,28},{28,24},{1,5},{5... | collective-permute-start | bytes 8650760 | tf_op jit(solution)/shard_map/ppermute | solution.py:94
  497.8 27.9 %collective-permute-start.23 = (bf16[256,2048]{1,0:T(8,128)(2,1)S(1)}, bf16[256,2048]{1,0:T(8,128)(2,1)S(1)}, u32[]{:S(2)}, u32[]{:S(2)}) collective-permute-start(bf16[256,2048]{1,0:T(8,128)(2,1)S(1)} %constant_dynamic-update-slice_fusion.9), channel_id=1, source_target_pairs={{0,4},{4,0},{8,12},{12,8},{16,20},{20,16},{24,28},{28,24},{1,5},{5... | collective-permute-start | bytes 3145736 | tf_op jit(solution)/shard_map/ppermute | solution.py:94
  503.5 17.4 %collective-permute-start.5 = (bf16[1024,512]{1,0:T(8,128)(2,1)S(1)}, bf16[1024,512]{1,0:T(8,128)(2,1)S(1)}, u32[]{:S(2)}, u32[]{:S(2)}) collective-permute-start(bf16[1024,512]{1,0:T(8,128)(2,1)S(1)} %constant_dynamic-update-slice_fusion.23), channel_id=1, source_target_pairs={{0,4},{4,0},{8,12},{12,8},{16,20},{20,16},{24,28},{28,24},{1,5},{5... | collective-permute-start | bytes 3145736 | tf_op jit(solution)/shard_map/ppermute | solution.py:94
  511.3 9.9 %collective-permute-start.11 = (bf16[1024,512]{1,0:T(8,128)(2,1)S(1)}, bf16[1024,512]{1,0:T(8,128)(2,1)}, u32[]{:S(2)}, u32[]{:S(2)}) collective-permute-start(bf16[1024,512]{1,0:T(8,128)(2,1)S(1)} %constant_dynamic-update-slice_fusion.18), channel_id=1, source_target_pairs={{0,4},{4,0},{8,12},{12,8},{16,20},{20,16},{24,28},{28,24},{1,5},{5... | collective-permute-start | bytes 3145736 | tf_op jit(solution)/shard_map/ppermute | solution.py:94
  516.5 6.9 %collective-permute-start.17 = (bf16[1024,512]{1,0:T(8,128)(2,1)S(1)}, bf16[1024,512]{1,0:T(8,128)(2,1)}, u32[]{:S(2)}, u32[]{:S(2)}) collective-permute-start(bf16[1024,512]{1,0:T(8,128)(2,1)S(1)} %constant_dynamic-update-slice_fusion.14), channel_id=1, source_target_pairs={{0,4},{4,0},{8,12},{12,8},{16,20},{20,16},{24,28},{28,24},{1,5},{5... | collective-permute-start | bytes 3145736 | tf_op jit(solution)/shard_map/ppermute | solution.py:94
  527.4 44.6 %copy-start.30 = (f32[128,2048]{1,0:T(8,128)S(1)}, f32[128,2048]{1,0:T(8,128)}, u32[]{:S(2)}) copy-start(f32[128,2048]{1,0:T(8,128)} %get-tuple-element.63) | copy-start | bytes 3145732
  (50 other events, 333.8 us)
Sparse Core Ops, SparseCore 0:
  155.4 42.1 reduce-scatter.5
  199.9 42.8 reduce-scatter.3
  314.9 43.5 all-gather.1
  404.2 42.5 reduce-scatter.7

commit v3 on v2

--- a/solution.py
+++ b/solution.py
@@ -30,45 +30,10 @@
     return inverse * (centred - scaled * jnp.mean(weighted * scaled, axis=-1, keepdims=True))
 
 
-def rotary_tables(length, rotated):
-    half_width = rotated // 2
-    frequency = rotary_base ** (-(jnp.arange(half_width, dtype=jnp.float32) * 2.0 / rotated))
-    angles = jnp.arange(length, dtype=jnp.float32)[:, None] * frequency[None, :]
-    cosine = jnp.concatenate([jnp.cos(angles), jnp.cos(angles)], axis=-1)
-    sine_table = jnp.concatenate([jnp.sin(angles), jnp.sin(angles)], axis=-1)
-    return (cosine[:, None, :], sine_table[:, None, :])
-
-
-def rotate(vector, cosine, sine_table):
-    rotated = cosine.shape[-1]
-    half_width = rotated // 2
-    leading = vector[..., :rotated]
-    turned = jnp.concatenate([-leading[..., half_width:], leading[..., :half_width]], axis=-1)
-    return jnp.concatenate([leading * cosine + turned * sine_table, vector[..., rotated:]], axis=-1)
-
-
-def rotate_back(grad_vec, cosine, sine_table):
-    rotated = cosine.shape[-1]
-    half_width = rotated // 2
-    leading = grad_vec[..., :rotated]
-    moved = leading * sine_table
-    turned = jnp.concatenate([moved[..., half_width:], -moved[..., :half_width]], axis=-1)
-    return jnp.concatenate([leading * cosine + turned, grad_vec[..., rotated:]], axis=-1)
-
-
 def product(left, right, left_dim, right_dim):
     return lax.dot_general(
         left, right, (((left_dim,), (right_dim,)), ((), ())), preferred_element_type=jnp.float32
     )
-
-
-def masked_scores(query, keys, scale):
-    length = query.shape[1]
-    scores = jnp.einsum("sqhd,skhd->shqk", query, keys, preferred_element_type=jnp.float32) * scale
-    causal = lax.broadcasted_iota(jnp.int32, (length, length), 0) >= lax.broadcasted_iota(
-        jnp.int32, (length, length), 1
-    )
-    return jnp.where(causal, scores, -1e30)
 
 
 def halving_masks(ways):
@@ -125,12 +90,6 @@
         return piece
 
 
-def scatter_sum(value):
-    return lax.psum_scatter(
-        value.astype(jnp.bfloat16), "tensor", scatter_dimension=0, tiled=True
-    ).astype(jnp.float32)
-
-
 MESH = pl.DeviceIdType.MESH
 
 
@@ -236,11 +195,12 @@
         self.send_sem, self.recv_sem = send_sem, recv_sem
 
     def copy(self, way, slot):
+        spot = slot + 1 - way
         return pltpu.make_async_remote_copy(
             src_ref=self.held.at[slot],
-            dst_ref=self.arrived.at[way, slot],
+            dst_ref=self.arrived.at[spot],
             send_sem=self.send_sem.at[slot],
-            recv_sem=self.recv_sem.at[way, slot],
+            recv_sem=self.recv_sem.at[spot],
             device_id={"tensor": self.place + 1 - 2 * way},
             device_id_type=MESH,
         )
@@ -248,35 +208,38 @@
     def has_source(self, way):
         return jnp.where(way == 0, self.place > 0, self.place < self.ways - 1)
 
-    def send_all(self, partial, between=None):
-        def step_body(i, carry):
-            step = self.ways - 1 - i
-
-            def side(way, inner_carry):
-                slot = jnp.where(way == 0, self.place + step, self.place - step)
-
-                @pl.when((slot >= 0) & (slot < self.ways))
+    def step(self, number, partial=None):
+        distance = self.ways - 1 - number
+
+        def side(way, carry):
+            slot = jnp.where(way == 0, self.place + distance, self.place - distance)
+
+            @pl.when((slot >= 0) & (slot < self.ways))
+            def _():
+                if partial is not None:
+                    self.held[slot] = partial(slot).astype(jnp.bfloat16)
+
+                @pl.when(self.has_source(way))
                 def _():
-                    self.held[slot] = partial(slot).astype(jnp.bfloat16)
-
-                    @pl.when(self.has_source(way))
-                    def _():
-                        self.copy(way, slot).wait_recv()
-                        self.held[slot] = (
-                            self.held[slot].astype(jnp.float32)
-                            + self.arrived[way, slot].astype(jnp.float32)
-                        ).astype(jnp.bfloat16)
-
-                    self.copy(way, slot).start()
-
-                return inner_carry
-
-            carry = lax.fori_loop(0, 2, side, carry)
-            if between is not None:
-                between(i)
+                    self.copy(way, slot).wait_recv()
+                    self.held[slot] = (
+                        self.held[slot].astype(jnp.float32)
+                        + self.arrived[slot + 1 - way].astype(jnp.float32)
+                    ).astype(jnp.bfloat16)
+
+                self.copy(way, slot).start()
+
             return carry
 
-        lax.fori_loop(0, self.ways - 1, step_body, 0)
+        lax.fori_loop(0, 2, side, 0)
+
+    def send_all(self, partial, between):
+        def one(number, carry):
+            self.step(number, partial)
+            between(number)
+            return carry
+
+        lax.fori_loop(0, self.ways - 1, one, 0)
 
     def finish(self, total):
         for way in range(2):
@@ -284,7 +247,7 @@
             @pl.when(self.has_source(way))
             def _():
                 self.copy(way, self.place).wait_recv()
-                total[...] += self.arrived[way, self.place].astype(jnp.float32)
+                total[...] += self.arrived[self.place + 1 - way].astype(jnp.float32)
 
     def drain(self):
         def one(slot, carry):
@@ -380,6 +343,8 @@
     hidden,
     grad_gate,
     grad_up,
+    partial_two,
+    partial_out,
     qkv_weight,
     out_weight,
     gate_weight,
@@ -481,10 +446,20 @@
         sigmoid = 1.0 / (1.0 + jnp.exp(-gate))
         gated = gate * sigmoid
         grad = grad_hidden[rows, :]
-        hidden[rows, :] = (gated * upward).astype(jnp.bfloat16)
-        grad_up[rows, :] = (grad * gated).astype(jnp.bfloat16)
-        grad_gate[rows, :] = (
-            grad * upward * sigmoid * (1.0 + gate * (1.0 - sigmoid))
+        low = [
+            piece.astype(jnp.bfloat16)
+            for piece in (
+                gated * upward,
+                grad * upward * sigmoid * (1.0 + gate * (1.0 - sigmoid)),
+                grad * gated,
+            )
+        ]
+        hidden[rows, :], grad_gate[rows, :], grad_up[rows, :] = low
+        partial_two[slot] = (
+            product(low[1], gate_weight[...], 1, 1) + product(low[2], up_weight[...], 1, 1)
+        ).astype(jnp.bfloat16)
+        partial_out[slot] = jnp.dot(
+            low[0], down_weight[...], preferred_element_type=jnp.float32
         ).astype(jnp.bfloat16)
 
     two.each(feed)
@@ -531,6 +506,8 @@
         low(group, units),
         low(group, units),
         low(group, units),
+        low(ways, size, width),
+        low(ways, size, width),
     )
     return pl.pallas_call(
         functools.partial(forward_kernel, ways, LEN),
@@ -545,12 +522,12 @@
             pltpu.VMEM(down_weight.shape, jnp.bfloat16),
             pltpu.VMEM((group, units), jnp.float32),
             pltpu.VMEM((ways, size, width), jnp.bfloat16),
-            pltpu.VMEM((2, ways, size, width), jnp.bfloat16),
+            pltpu.VMEM((ways + 1, size, width), jnp.bfloat16),
             pltpu.SemaphoreType.DMA((5,)),
             pltpu.SemaphoreType.DMA((3, 2, ways)),
             pltpu.SemaphoreType.DMA((3, ways)),
             pltpu.SemaphoreType.DMA((ways,)),
-            pltpu.SemaphoreType.DMA((2, ways)),
+            pltpu.SemaphoreType.DMA((ways + 1,)),
         ],
         compiler_params=pltpu.CompilerParams(
             collective_id=0, has_side_effects=True, vmem_limit_bytes=67043328
@@ -567,6 +544,508 @@
         up_weight,
         down_weight,
     )
+
+
+class Cross:
+    def __init__(self, ways):
+        self.ways = ways
+        self.place = lax.axis_index("dp")
+        self.levels = ways.bit_length() - 1
+        odd = lax.rem(self.place, 2)
+        even_masks, odd_masks = halving_masks(ways)
+        self.keeps, self.partners, self.offsets, self.sizes = [], [], [], []
+        offset, size = 0, ways
+        for even_mask, odd_mask in zip(even_masks, odd_masks):
+            mask = even_mask + (odd_mask - even_mask) * odd
+            keep = lax.rem(self.place // mask, 2)
+            size //= 2
+            offset = offset + keep * size
+            self.keeps.append(keep)
+            self.partners.append(self.place + mask * (1 - 2 * keep))
+            self.offsets.append(offset)
+            self.sizes.append(size)
+
+    def away(self, level):
+        start = self.offsets[level - 1] if level > 0 else 0
+        return start + (1 - self.keeps[level]) * self.sizes[level]
+
+
+class Exchange:
+    def __init__(self, cross, by_rows, unit, left, right, sends, gots, whole, loaded, sems):
+        self.cross, self.by_rows, self.unit = cross, by_rows, unit
+        self.left, self.right = left, right
+        self.sends, self.gots, self.whole, self.loaded = sends, gots, whole, loaded
+        self.send_sem, self.recv_sem, self.local_sem = sems
+
+    def span(self, start, count):
+        size = count * self.unit
+        where = start * self.unit
+        where = where if isinstance(where, int) else pl.multiple_of(where, self.unit)
+        return pl.ds(where, size)
+
+    def view(self, ref, start, count):
+        if self.by_rows:
+            return ref.at[self.span(start, count), :]
+        return ref.at[:, self.span(start, count)]
+
+    def remote(self, source, target, level, phase):
+        index = phase * self.cross.levels + level
+        return pltpu.make_async_remote_copy(
+            src_ref=source,
+            dst_ref=target,
+            send_sem=self.send_sem.at[index],
+            recv_sem=self.recv_sem.at[index],
+            device_id={"dp": self.cross.partners[level]},
+            device_id_type=MESH,
+        )
+
+    def halving(self, level):
+        return self.remote(self.sends[level], self.gots[level], level, 0)
+
+    def reduce(self, level):
+        cross = self.cross
+        last = level == cross.levels
+        start = cross.offsets[-1] if last else cross.away(level)
+        count = 1 if last else cross.sizes[level]
+        if level > 0:
+            self.halving(level - 1).wait_recv()
+        target = self.sends[level]
+
+        def one(i, carry):
+            loads = []
+            for j in range(level):
+                load = pltpu.make_async_copy(
+                    self.view(self.gots[j], start + i - cross.offsets[j], 1),
+                    self.loaded.at[j],
+                    self.local_sem.at[j],
+                )
+                load.start()
+                loads.append(load)
+            place = self.span(start + i, 1)
+            if self.by_rows:
+                total = product(self.left[:, place], self.right[...], 0, 0)
+            else:
+                total = jnp.dot(
+                    self.left[...], self.right[:, place], preferred_element_type=jnp.float32
+                )
+            for j, load in enumerate(loads):
+                load.wait()
+                total = total + self.loaded[j].astype(jnp.float32)
+            spot = self.span(i, 1)
+            if self.by_rows:
+                target[spot, :] = total.astype(jnp.bfloat16)
+            else:
+                target[:, spot] = total.astype(jnp.bfloat16)
+            return carry
+
+        if count == 1:
+            one(0, 0)
+        else:
+            lax.fori_loop(0, count, one, 0)
+        if not last:
+            self.halving(level).start()
+
+    def doubling(self, level):
+        cross = self.cross
+        spot = self.view(self.whole, cross.offsets[level], cross.sizes[level])
+        source = self.sends[cross.levels] if level == cross.levels - 1 else spot
+        return self.remote(source, spot, level, 1)
+
+    def keep_unit(self):
+        return pltpu.make_async_copy(
+            self.sends[self.cross.levels],
+            self.view(self.whole, self.cross.offsets[-1], 1),
+            self.local_sem.at[self.cross.levels],
+        )
+
+    def spread(self, level):
+        if level == self.cross.levels - 1:
+            self.keep_unit().start()
+        else:
+            if level == self.cross.levels - 2:
+                self.keep_unit().wait()
+            self.doubling(level + 1).wait_recv()
+        self.doubling(level).start()
+
+    def drain(self):
+        self.doubling(0).wait_recv()
+        for level in range(self.cross.levels):
+            self.halving(level).wait_send()
+            self.doubling(level).wait_send()
+
+
+def norm_terms(values):
+    center = jnp.mean(values, axis=-1, keepdims=True)
+    offset = values - center
+    inverse = lax.rsqrt(jnp.mean(offset * offset, axis=-1, keepdims=True) + epsilon)
+    return offset * inverse, inverse
+
+
+def attention_back_tile(
+    length, base, tile, query, keys, values, mixed, logsum, grad_mixed, tables, grad_flat, sums, rows_of
+):
+    grad_query, grad_keys, grad_values = rows_of
+    columns = pl.ds(pl.multiple_of(tile * 128, 128), 128)
+    scale = HD ** (-0.5)
+    block = length // 2
+    for part in reversed(range(2)):
+        first = part * block
+        span = first + block
+        rows = pl.ds(base + first, block)
+        past = pl.ds(base, span)
+        here, incoming = query[rows, columns], grad_mixed[rows, columns]
+        lane = lax.broadcasted_iota(jnp.int32, here.shape, 1)
+        causal = (
+            lax.broadcasted_iota(jnp.int32, (block, span), 0) + first
+            >= lax.broadcasted_iota(jnp.int32, (block, span), 1)
+        )
+        dots = incoming.astype(jnp.float32) * mixed[rows, columns].astype(jnp.float32)
+        logs = logsum[rows, :]
+        past_keys, past_values = keys[past, columns], values[past, columns]
+        key_lane = lax.broadcasted_iota(jnp.int32, past_keys.shape, 1)
+        totals = [0.0, 0.0, 0.0]
+        for head in range(2):
+            mine = (lane // HD) == head
+            own_query = jnp.where(mine, here, 0)
+            own_grad = jnp.where(mine, incoming, 0)
+            log = jnp.sum(jnp.where(lane == 2 * tile + head, logs, 0.0), axis=-1, keepdims=True)
+            delta = jnp.sum(jnp.where(mine, dots, 0.0), axis=-1, keepdims=True)
+            scores = product(own_query, past_keys, 1, 1) * scale
+            probs = jnp.where(causal, jnp.exp(scores - log), 0.0)
+            grad_weights = product(own_grad, past_values, 1, 1)
+            grad_scores = (probs * (grad_weights - delta) * scale).astype(jnp.bfloat16)
+            own_keys = jnp.where((key_lane // HD) == head, past_keys, 0)
+            terms = (
+                jnp.dot(grad_scores, own_keys, preferred_element_type=jnp.float32),
+                product(grad_scores, own_query, 0, 0),
+                product(probs.astype(jnp.bfloat16), own_grad, 0, 0),
+            )
+            totals = [total + term for total, term in zip(totals, terms)]
+        grad_query[pl.ds(first, block), :] = totals[0]
+        for target, total in ((grad_keys, totals[1]), (grad_values, totals[2])):
+            if part == 1:
+                target[...] = total
+            else:
+                target[pl.ds(0, span), :] += total
+    inner = query.shape[1]
+    every = pl.ds(base, length)
+    for i, target in enumerate(rows_of):
+        result = target[...]
+        if i < 2:
+            result = turn_pairs(result, *(table[...] for table in tables), -1.0)
+        sums[pl.ds(4 + i, 1), columns] += jnp.sum(result, axis=0, keepdims=True)
+        spot = pl.ds(pl.multiple_of(i * inner + tile * 128, 128), 128)
+        grad_flat[every, spot] = result.astype(jnp.bfloat16)
+
+
+def backward_kernel(ways, tensor_ways, length, count, *refs):
+    (
+        block_input,
+        cotangent,
+        norm1_gain,
+        norm2_gain,
+        cosine,
+        sine_low,
+        sine_high,
+        attended,
+        *hbm,
+    ) = refs[: 8 + count]
+    (
+        partial_two_hbm,
+        partial_out_hbm,
+        grad_rows_hbm,
+        hidden_hbm,
+        rows_two_hbm,
+        grad_gate_hbm,
+        grad_up_hbm,
+        out_weight_hbm,
+        query_hbm,
+        keys_hbm,
+        values_hbm,
+        mixed_hbm,
+        logsum_hbm,
+        qkv_weight_hbm,
+    ) = hbm
+    levels = ways.bit_length() - 1
+    rest = list(refs[8 + count :])
+    take = lambda number: [rest.pop(0) for _ in range(number)]
+    block_output, input_grad, sums, grad_low_rows, grad_flat, down_whole, gate_whole, up_whole = take(8)
+    down_got, gate_got, up_got = take(levels), take(levels), take(levels)
+    held_two, held_out, grad_rows, rows_two, grad_gate, grad_up, out_weight = take(7)
+    query, keys, values, mixed, logsum, qkv_weight = take(6)
+    down_send, gate_send, up_send = take(levels + 1), take(levels + 1), take(levels + 1)
+    down_loaded, feed_loaded = take(2)
+    hidden = gate_send[0].at[pl.ds(0, hidden_hbm.shape[0])]
+    hidden_turned, arrived_two, arrived_out, grad_mixed, stream_grad = take(5)
+    tile_rows = take(3)
+    (swapped,) = take(1)
+    load_sem, gather_send, gather_recv, scatter_send, scatter_recv = take(5)
+    send_sem, recv_sem, local_sem, small_send, small_recv = take(5)
+    place = lax.axis_index("tensor")
+    targets = (
+        held_two,
+        held_out,
+        grad_rows,
+        hidden,
+        rows_two,
+        grad_gate,
+        grad_up,
+        out_weight,
+        query,
+        keys,
+        values,
+        mixed,
+        logsum,
+        qkv_weight,
+    )
+    order = (0, 2, 3, 4, 5, 6, 7, 8, 9, 10, 11, 12, 13, 1)
+    loads = [
+        pltpu.make_async_copy(source, target, load_sem.at[i])
+        for i, (source, target) in enumerate(zip(hbm, targets))
+    ]
+    for i in order:
+        loads[i].start()
+    cross = Cross(ways)
+    tensor_levels = tensor_ways.bit_length() - 1
+    tensor_partners = []
+    for level in range(tensor_levels):
+        bit = lax.rem(place // (1 << level), 2)
+        tensor_partners.append(place + (1 << level) * (1 - 2 * bit))
+    barrier = pltpu.get_barrier_semaphore()
+    for step, there in ((-1, place > 0), (1, place < tensor_ways - 1)):
+
+        @pl.when(there)
+        def _():
+            pl.semaphore_signal(
+                barrier, inc=1, device_id={"tensor": place + step}, device_id_type=MESH
+            )
+
+    for partner in cross.partners:
+        pl.semaphore_signal(barrier, inc=1, device_id={"dp": partner}, device_id_type=MESH)
+    for partner in tensor_partners[1:]:
+        pl.semaphore_signal(barrier, inc=1, device_id={"tensor": partner}, device_id_type=MESH)
+    pl.semaphore_wait(
+        barrier,
+        (place > 0).astype(jnp.int32)
+        + (place < tensor_ways - 1).astype(jnp.int32)
+        + (levels + tensor_levels - 1),
+    )
+    size, width = block_input.shape
+    unit = width // ways
+    sems = lambda i: (send_sem.at[i], recv_sem.at[i], local_sem.at[i])
+    down = Exchange(
+        cross, False, unit, hidden_turned, grad_rows, down_send, down_got, down_whole, down_loaded, sems(0)
+    )
+    gate = Exchange(
+        cross, True, unit, rows_two, grad_gate, gate_send, gate_got, gate_whole, feed_loaded, sems(1)
+    )
+    up = Exchange(cross, True, unit, rows_two, grad_up, up_send, up_got, up_whole, feed_loaded, sems(2))
+    two = LineScatter(
+        held_two, arrived_two, place, tensor_ways, scatter_send.at[0], scatter_recv.at[0]
+    )
+    out = LineScatter(
+        held_out, arrived_out, place, tensor_ways, scatter_send.at[1], scatter_recv.at[1]
+    )
+    one = LineScatter(
+        held_two, arrived_two, place, tensor_ways, scatter_send.at[2], scatter_recv.at[2]
+    )
+    low = LineGather(grad_low_rows, place, tensor_ways, gather_send, gather_recv)
+    own = pl.ds(pl.multiple_of(place * size, size), size)
+
+    loads[0].wait()
+    two.step(0)
+    loads[2].wait()
+    loads[3].wait()
+    hidden_turned[...] = hidden[...].T
+    down.reduce(0)
+    loads[4].wait()
+    loads[5].wait()
+    gate.reduce(0)
+    down.reduce(1)
+    two.step(1)
+    loads[6].wait()
+    up.reduce(0)
+    gate.reduce(1)
+    up.reduce(1)
+    for step in range(2, tensor_ways - 1):
+        two.step(step)
+    down.reduce(2)
+    stream_grad[...] = held_two[place].astype(jnp.float32)
+    two.finish(stream_grad)
+
+    scaled, inverse = norm_terms(attended[...])
+    grad = stream_grad[...]
+    sums[...] = jnp.zeros_like(sums)
+    sums[pl.ds(2, 1), :] = jnp.sum(grad * scaled, axis=0, keepdims=True)
+    sums[pl.ds(3, 1), :] = jnp.sum(grad, axis=0, keepdims=True)
+    stream_grad[...] = cotangent[...].astype(jnp.float32) + norm_back(
+        grad, scaled, inverse, norm2_gain[...]
+    )
+    grad_low_rows[own, :] = stream_grad[...].astype(jnp.bfloat16)
+    low.start()
+    two.drain()
+    for level in range(3, levels + 1):
+        down.reduce(level)
+    down.spread(levels - 1)
+    gate.reduce(2)
+    loads[7].wait()
+
+    def turn_back(slot):
+        rows = pl.ds(pl.multiple_of(slot * size, size), size)
+        grad_mixed[rows, :] = product(grad_low_rows[rows, :], out_weight[...], 1, 1).astype(
+            jnp.bfloat16
+        )
+
+    low.hop(1)
+    up.reduce(2)
+    down.spread(levels - 2)
+    for level in range(3, levels + 1):
+        gate.reduce(level)
+    gate.spread(levels - 1)
+    low.hop(2)
+    for level in range(3, levels + 1):
+        up.reduce(level)
+    up.spread(levels - 1)
+    gate.spread(levels - 2)
+    for step in range(3, tensor_ways):
+        low.hop(step)
+    low.each(turn_back, False)
+    for level in range(levels - 3, -1, -1):
+        down.spread(level)
+    for i in range(8, 14):
+        loads[i].wait()
+    tiles = query.shape[1] // 128
+
+    def attend(i, carry):
+        base = pl.multiple_of((i // tiles) * length, length)
+        attention_back_tile(
+            length,
+            base,
+            lax.rem(i, tiles),
+            query,
+            keys,
+            values,
+            mixed,
+            logsum,
+            grad_mixed,
+            (cosine, sine_low, sine_high),
+            grad_flat,
+            sums,
+            tile_rows,
+        )
+        return carry
+
+    lax.fori_loop(0, tiles * (query.shape[0] // length), attend, 0)
+    inner = query.shape[1]
+
+    def part(slot):
+        rows = pl.ds(pl.multiple_of(slot * size, size), size)
+        return sum(
+            product(grad_flat[rows, i * inner : (i + 1) * inner], qkv_weight[i], 1, 1)
+            for i in range(3)
+        )
+
+    up.spread(levels - 2)
+    one.step(0, part)
+    for level in range(levels - 3, -1, -1):
+        gate.spread(level)
+    loads[1].wait()
+    for step in range(1, tensor_ways - 1):
+        one.step(step, part)
+        out.step(step - 1)
+    input_grad[...] = part(place)
+    one.finish(input_grad)
+    out.step(tensor_ways - 2)
+    scaled, inverse = norm_terms(block_input[...].astype(jnp.float32))
+    grad = input_grad[...]
+    sums[pl.ds(0, 1), :] = jnp.sum(grad * scaled, axis=0, keepdims=True)
+    sums[pl.ds(1, 1), :] = jnp.sum(grad, axis=0, keepdims=True)
+    input_grad[...] = stream_grad[...] + norm_back(grad, scaled, inverse, norm1_gain[...])
+    for level in range(levels - 3, -1, -1):
+        up.spread(level)
+    peers = [("dp", partner) for partner in cross.partners]
+    peers += [("tensor", partner) for partner in tensor_partners]
+    for i, (axis, partner) in enumerate(peers):
+        rows = pl.ds(0, 8 if axis == "dp" else 4)
+        swap = pltpu.make_async_remote_copy(
+            src_ref=sums.at[rows],
+            dst_ref=swapped.at[i, rows],
+            send_sem=small_send.at[i],
+            recv_sem=small_recv.at[i],
+            device_id={axis: partner},
+            device_id_type=MESH,
+        )
+        swap.start()
+        swap.wait()
+        sums[rows, :] += swapped[i, rows]
+    stream_grad[...] = held_out[place].astype(jnp.float32)
+    out.finish(stream_grad)
+    block_output[...] = (attended[...] + stream_grad[...]).astype(jnp.bfloat16)
+    low.drain()
+    one.drain()
+    out.drain()
+    for exchange in (down, gate, up):
+        exchange.drain()
+
+
+def backward(ways, tensor_ways, resident, streamed, shapes):
+    size, width, inner, units = shapes
+    group = size * tensor_ways
+    levels = ways.bit_length() - 1
+    unit = width // ways
+    low = lambda *shape: jax.ShapeDtypeStruct(shape, jnp.bfloat16)
+    full = lambda *shape: jax.ShapeDtypeStruct(shape, jnp.float32)
+    vmem = pl.BlockSpec(memory_space=pltpu.VMEM)
+    hbm = pl.BlockSpec(memory_space=pl.ANY)
+    halves = [ways >> (level + 1) for level in range(levels)]
+    by_columns = lambda number: (units, number * unit)
+    by_rows = lambda number: (number * unit, units)
+    results = [
+        low(size, width),
+        full(size, width),
+        full(8, width),
+        low(group, width),
+        low(group, 3 * inner),
+    ]
+    distant = [low(units, width), low(width, units), low(width, units)]
+    for form in (by_columns, by_rows, by_rows):
+        distant += [low(*form(number)) for number in halves]
+    scratch = [
+        pltpu.VMEM(array.shape, array.dtype) for i, array in enumerate(streamed) if i != 3
+    ]
+    for form in (by_columns, by_rows, by_rows):
+        scratch += [pltpu.VMEM(form(number), jnp.bfloat16) for number in halves + [1]]
+    scratch += [
+        pltpu.VMEM((levels,) + by_columns(1), jnp.bfloat16),
+        pltpu.VMEM((levels,) + by_rows(1), jnp.bfloat16),
+        pltpu.VMEM((units, group), jnp.bfloat16),
+        pltpu.VMEM((tensor_ways + 1, size, width), jnp.bfloat16),
+        pltpu.VMEM((tensor_ways + 1, size, width), jnp.bfloat16),
+        pltpu.VMEM((group, inner), jnp.bfloat16),
+        pltpu.VMEM((size, width), jnp.float32),
+        *[pltpu.VMEM((LEN, 128), jnp.float32)] * 3,
+        pltpu.VMEM((levels + tensor_ways.bit_length() - 1, 8, width), jnp.float32),
+        pltpu.SemaphoreType.DMA((len(streamed),)),
+        pltpu.SemaphoreType.DMA((2, tensor_ways)),
+        pltpu.SemaphoreType.DMA((tensor_ways,)),
+        pltpu.SemaphoreType.DMA((3, tensor_ways)),
+        pltpu.SemaphoreType.DMA((3, tensor_ways + 1)),
+        pltpu.SemaphoreType.DMA((3, 2 * levels)),
+        pltpu.SemaphoreType.DMA((3, 2 * levels)),
+        pltpu.SemaphoreType.DMA((3, levels + 1)),
+        pltpu.SemaphoreType.DMA((levels + tensor_ways.bit_length() - 1,)),
+        pltpu.SemaphoreType.DMA((levels + tensor_ways.bit_length() - 1,)),
+    ]
+    return pl.pallas_call(
+        functools.partial(backward_kernel, ways, tensor_ways, LEN, len(streamed)),
+        out_shape=results + distant,
+        in_specs=[vmem] * len(resident) + [hbm] * len(streamed),
+        out_specs=[vmem] * len(results) + [hbm] * len(distant),
+        scratch_shapes=scratch,
+        compiler_params=pltpu.CompilerParams(
+            collective_id=1, has_side_effects=True, vmem_limit_bytes=67043328
+        ),
+    )(*resident, *streamed)[:8]
 
 
 def body(
@@ -585,14 +1064,12 @@
     down_weight,
     cotangent,
 ):
-    width = block_input.shape[1]
-    inner = qkv_weight.shape[2]
-    local_heads = inner // HD
-    scale = HD ** (-0.5)
-    parts = [qkv_weight[:, i] for i in range(3)]
+    size, width = block_input.shape
+    inner, units = qkv_weight.shape[2], gate_weight.shape[1]
     halver = Halver("dp", ways)
-    cosine, sine_table = rotary_tables(LEN, ROT)
-    stream = block_input.astype(jnp.float32)
+    turned = jnp.transpose(qkv_weight, (1, 0, 2))
+    tables = rotary_lanes(LEN)
+    row = lambda vector: vector.reshape(1, width)
     (
         rows_one,
         query,
@@ -606,91 +1083,49 @@
         hidden,
         grad_gate,
         grad_up,
+        partial_two,
+        partial_out,
     ) = forward(
         tensor_ways,
         block_input,
         cotangent,
-        [row.reshape(1, width) for row in (norm1_gain, norm1_bias, norm2_gain, norm2_bias)],
-        jnp.transpose(qkv_weight, (1, 0, 2)),
+        [row(vector) for vector in (norm1_gain, norm1_bias, norm2_gain, norm2_bias)],
+        turned,
         qkv_bias,
-        rotary_lanes(LEN),
+        tables,
         (out_weight, gate_weight, up_weight, down_weight),
     )
-    group = rows_one.shape[0]
-    seq_count = group // LEN
-    query, keys, values, mixed_heads = (
-        piece.reshape(seq_count, LEN, local_heads, HD) for piece in (query, keys, values, mixed)
-    )
-    logsum = jnp.transpose(logsum[:, :local_heads].reshape(seq_count, LEN, local_heads), (0, 2, 1))
-    logsum = logsum[..., None]
-    _, scaled_one, inverse_one = layer_norm(stream, norm1_gain, norm1_bias)
-    _, scaled_two, inverse_two = layer_norm(attended, norm2_gain, norm2_bias)
-    block_output = (
-        attended + scatter_sum(jnp.dot(hidden, down_weight, preferred_element_type=jnp.float32))
-    ).astype(jnp.bfloat16)
-    grad_normed_two = scatter_sum(
-        product(grad_gate, gate_weight, 1, 1) + product(grad_up, up_weight, 1, 1)
-    )
-    down_piece = halver.reduce(hidden, grad_rows)
-    gate_piece = halver.reduce(rows_two, grad_gate)
-    up_piece = halver.reduce(rows_two, grad_up)
-    norm2_gain_part = jnp.sum(grad_normed_two * scaled_two, axis=0)
-    norm2_bias_part = jnp.sum(grad_normed_two, axis=0)
-    grad_stream = cotangent.astype(jnp.float32) + norm_back(
-        grad_normed_two, scaled_two, inverse_two, norm2_gain
-    )
-    grad_low = grad_stream.astype(jnp.bfloat16)
-    grad_attended = lax.all_gather(grad_low, "tensor", axis=0, tiled=True)
-    out_piece = halver.reduce(mixed, grad_attended)
-    grad_mixed = (
-        product(grad_attended, out_weight, 1, 1)
-        .astype(jnp.bfloat16)
-        .reshape(seq_count, LEN, local_heads, HD)
-    )
-    scores = masked_scores(query, keys, scale)
-    probs = jnp.exp(scores - logsum)
-    weights = probs.astype(jnp.bfloat16)
-    delta = jnp.einsum(
-        "sqhd,sqhd->shq", grad_mixed, mixed_heads, preferred_element_type=jnp.float32
-    )[..., None]
-    grad_weights = jnp.einsum(
-        "sqhd,skhd->shqk", grad_mixed, values, preferred_element_type=jnp.float32
-    )
-    grad_scores = (probs * (grad_weights - delta) * scale).astype(jnp.bfloat16)
-    grad_query = jnp.einsum(
-        "shqk,skhd->sqhd", grad_scores, keys, preferred_element_type=jnp.float32
-    )
-    grad_keys = jnp.einsum(
-        "shqk,sqhd->skhd", grad_scores, query, preferred_element_type=jnp.float32
-    )
-    grad_values = jnp.einsum(
-        "shqk,sqhd->skhd", weights, grad_mixed, preferred_element_type=jnp.float32
-    )
-    grad_projected = [
-        piece.reshape(group, inner)
-        for piece in (
-            rotate_back(grad_query, cosine, sine_table),
-            rotate_back(grad_keys, cosine, sine_table),
-            grad_values,
-        )
-    ]
-    bias_grad = jnp.stack([jnp.sum(piece, axis=0) for piece in grad_projected])
-    grad_flat = [piece.astype(jnp.bfloat16) for piece in grad_projected]
-    grad_normed_one = scatter_sum(
-        sum(product(piece, part, 1, 1) for piece, part in zip(grad_flat, parts))
-    )
-    qkv_pieces = [halver.reduce(rows_one, piece) for piece in grad_flat]
-    norm1_gain_part = jnp.sum(grad_normed_one * scaled_one, axis=0)
-    norm1_bias_part = jnp.sum(grad_normed_one, axis=0)
-    input_grad = grad_stream + norm_back(grad_normed_one, scaled_one, inverse_one, norm1_gain)
-    norm1_gain_grad, norm1_bias_grad, norm2_gain_grad, norm2_bias_grad = lax.psum(
-        (norm1_gain_part, norm1_bias_part, norm2_gain_part, norm2_bias_part), ("dp", "tensor")
-    )
-    bias_grad = lax.psum(bias_grad, "dp")
-    down_grad, gate_grad, up_grad, out_grad = (
-        halver.spread(piece) for piece in (down_piece, gate_piece, up_piece, out_piece)
-    )
-    qkv_grad = jnp.stack([halver.spread(piece) for piece in qkv_pieces], axis=1)
+    block_output, input_grad, sums, grad_low_rows, grad_flat, *wholes = backward(
+        ways,
+        tensor_ways,
+        [block_input, cotangent, row(norm1_gain), row(norm2_gain), *tables, attended],
+        [
+            partial_two,
+            partial_out,
+            grad_rows,
+            hidden,
+            rows_two,
+            grad_gate,
+            grad_up,
+            out_weight,
+            query,
+            keys,
+            values,
+            mixed,
+            logsum,
+            turned,
+        ],
+        (size, width, inner, units),
+    )
+    down_grad, gate_grad, up_grad = (whole.astype(jnp.float32) for whole in wholes)
+    qkv_piece = halver.reduce(rows_one, grad_flat)
+    out_piece = halver.reduce(mixed, grad_low_rows)
+    qkv_grad = halver.spread(qkv_piece).reshape(width, 3, inner)
+    out_grad = halver.spread(out_piece)
+    norm1_gain_grad, norm1_bias_grad, norm2_gain_grad, norm2_bias_grad = (
+        sums[i] for i in range(4)
+    )
+    bias_grad = sums[4:7, :inner]
     return (
         block_output,
         input_grad,

time: 589 us -> 536 us (0.910)
  Pallas kernels: 130 us -> 354 us
  matrix products: 122 us -> 20 us
  blocking collectives: 54 us -> 0 us
  waiting for transfers between devices: 110 us -> 65.7 us
  starting transfers between devices: 37.6 us -> 4.41 us
  other arithmetic: 59.6 us -> 41 us
  between operations: 15.5 us -> 1.07 us
  local copies, waits for them, and re-layouts: 52.7 us -> 43.7 us
    pallas_call x0 -> x1, Pallas kernels: none -> 214 us  [backward(): pl.pallas_call(functools.partial(backward_kernel, ways, tensor_ways, LEN,...]
    dot_general x34 -> x8, matrix products: 98.2 us -> 20 us  [product(): lax.dot_general(left, right, (((left_dim,), (right_dim,)), ((), ())), pre...]
    psum x2 -> x0, blocking collectives: 54 us -> none  [the longest x1 37.9 us: body(): lax.psum((norm1_gain_part, norm1_bias_part, norm2_gain_part, norm2_bias_p...]
    ppermute x42 -> x12, waiting for transfers between devices: 110 us -> 65.7 us  [swap(): return lax.ppermute(value, self.axis, pairs)]
    ppermute x42 -> x12, starting transfers between devices: 36.7 us -> 4.41 us  [swap(): return lax.ppermute(value, self.axis, pairs)]
    dot_general x6 -> x0, matrix products: 23.4 us -> none  [the longest x1 7.39 us: body(): jnp.dot(hidden, down_weight, preferred_element_type=jnp.float32)]
    convert_element_type x3 -> x4, other arithmetic: 3.3 us -> 23.9 us  [the longest x3 21.9 us: body(): whole.astype(jnp.float32)]
    dynamic_update_slice x14 -> x3, other arithmetic: 25.8 us -> 7.98 us  [spread(): lax.dynamic_update_slice_in_dim(whole, piece.astype(kind), keep * size, 0)]
  transfers between devices with their start and end apart: 46 -> 12, of which waited for: 19 -> 7; matrix products, arithmetic and copies ran while one was open for 36% -> 13% of each run, Pallas kernels for 0% -> 0%
where the time goes in v3:
time: 536 us; the launch traced here: 530 us
  Pallas kernels  354 us (66%)
  waiting for transfers between devices  65.7 us (12%)
  local copies, waits for them, and re-layouts  43.7 us (8%)
  other arithmetic  41 us (8%)
  matrix products  20 us (4%)
    pallas_call x1, Pallas kernels, backward(): pl.pallas_call(functools.partial(backward_kernel, ways, tensor_ways, LEN,...  214 us
    pallas_call x1, Pallas kernels, forward(): pl.pallas_call(functools.partial(forward_kernel, ways, LEN), out_shape=sh...  140 us
    ppermute x12, waiting for transfers between devices, swap(): return lax.ppermute(value, self.axis, pairs)  65.7 us
    convert_element_type x3, other arithmetic, body(): whole.astype(jnp.float32)  21.9 us
    dot_general x8, matrix products, product(): lax.dot_general(left, right, (((left_dim,), (right_dim,)), ((), ())), pre...  20 us
    unnamed x21, local copies, waits for them, and re-layouts  14.7 us
    broadcast_in_dim x6, local copies, waits for them, and re-layouts, spread(): whole = jnp.zeros((2 * size,) + piece.shape[1:], kind)  12.2 us
  transfers between devices with their start and end apart: 12, of which 7 were waited for; matrix products, arithmetic and copies ran while one was open for 13% of the time, Pallas kernels for 0%

profile of v3, /device:TPU:0, one launch (start us, length us, event | category | flops | bytes accessed | tf_op | source)
XLA Modules:
  0.0 530.1 jit_solution(9857183120118225794)
XLA Ops:
  0.7 1.0 fusion.12
  1.7 1.1 concatenate.16.sine_low.refs_5_
  2.8 1.1 concatenate.17.sine_high.refs_6_
  4.0 1.1 concatenate.15.cosine.refs_4_
  5.1 140.0 %shard_map.211 = (bf16[512,2048]{1,0:T(8,128)(2,1)}, bf16[512,512]{1,0:T(8,128)(2,1)}, bf16[512,512]{1,0:T(8,128)(2,1)}, bf16[512,512]{1,0:T(8,128)(2,1)}, f32[5...) custom-call(bf16[128,2048]{1,0:T(8,128)(2,1)} %refs_0_.1, ...), custom_call_target="tpu_custom_call" | custom-call | tf_op jit(solution)/shard_map/pallas_call | solution.py:512
  145.1 214.2 %shard_map.212 = (bf16[128,2048]{1,0:T(8,128)(2,1)}, f32[128,2048]{1,0:T(8,128)}, f32[8,2048]{1,0:T(8,128)}, bf16[512,2048]{1,0:T(8,128)(2,1)}, bf16[512,1536]{1...) custom-call(bf16[128,2048]{1,0:T(8,128)(2,1)} %refs_0_.1, ...), custom_call_target="tpu_custom_call" | custom-call | tf_op jit(solution)/shard_map/pallas_call | solution.py:1039
  359.3 5.3 %convolution_convert_fusion = bf16[1024,1536]{1,0:T(8,128)(2,1)} fusion(bf16[512,1536]{1,0:T(8,128)(2,1)} %get-tuple-element.51, bf16[512,2048]{1,0:T(8,128)(2,1)} %get-tuple-element.50, s32[]{:T(128)S(6)} %select_n.115), kind=kOutput, calls=%fused_computation.2 | convolution fusion | flops 1612185600 | bytes 5767172 | tf_op jit(solution)/shard_map/dot_general | solution.py:34
  364.6 6.0 %collective-permute-done = bf16[1024,1536]{1,0:T(8,128)(2,1)} collective-permute-done((bf16[1024,1536]{1,0:T(8,128)(2,1)}, bf16[1024,1536]{1,0:T(8,128)(2,1)}, u32[]{:S(2)}, u32[]{:S(2)}) %collective-permute-start) | collective-permute-done | bytes 3145760 | tf_op jit(solution)/shard_map/ppermute | solution.py:59
  370.6 3.7 add_convert_fusion
  374.4 20.7 %collective-permute-done.1 = bf16[512,1536]{1,0:T(8,128)(2,1)} collective-permute-done((bf16[512,1536]{1,0:T(8,128)(2,1)}, bf16[512,1536]{1,0:T(8,128)(2,1)}, u32[]{:S(2)}, u32[]{:S(2)}) %collective-permute-start.1) | collective-permute-done | bytes 1572896 | tf_op jit(solution)/shard_map/ppermute | solution.py:59
  395.1 2.6 add_convert_fusion.2
  397.8 1.7 convolution_convert_fusion.1
  399.5 2.1 fusion.10
  401.6 8.2 %collective-permute-done.2 = bf16[256,1536]{1,0:T(8,128)(2,1)} collective-permute-done((bf16[256,1536]{1,0:T(8,128)(2,1)S(1)}, bf16[256,1536]{1,0:T(8,128)(2,1)}, u32[]{:S(2)}, u32[]{:S(2)}) %collective-permute-start.2) | collective-permute-done | bytes 786464 | tf_op jit(solution)/shard_map/ppermute | solution.py:59
  409.8 2.0 add_convert_fusion.1
  411.9 2.3 add_convert_fusion.3
  414.3 1.2 collective-permute-start.7
  415.4 1.2 copy.24
  416.6 1.2 broadcast_in_dim.30
  418.0 0.9 constant_dynamic-update-slice_fusion.7
  418.9 10.7 %collective-permute-done.3 = bf16[256,1536]{1,0:T(8,128)(2,1)} collective-permute-done((bf16[256,1536]{1,0:T(8,128)(2,1)S(1)}, bf16[256,1536]{1,0:T(8,128)(2,1)}, u32[]{:S(2)}, u32[]{:S(2)}) %collective-permute-start.3) | collective-permute-done | bytes 786464 | tf_op jit(solution)/shard_map/ppermute | solution.py:59
  429.6 1.4 copy.25
  431.0 0.9 constant_dynamic-update-slice_fusion.6
  432.0 1.6 add_convert_fusion.5
  433.6 1.5 collective-permute-start.8
  435.7 7.2 %collective-permute-done.8 = bf16[64,2048]{1,0:T(8,128)(2,1)S(1)} collective-permute-done((bf16[64,2048]{1,0:T(8,128)(2,1)S(1)}, bf16[64,2048]{1,0:T(8,128)(2,1)S(1)}, u32[]{:S(2)}, u32[]{:S(2)}) %collective-permute-start.8) | collective-permute-done | bytes 262176 | tf_op jit(solution)/shard_map/ppermute | solution.py:59
  442.9 0.8 broadcast_in_dim.33
  443.7 1.8 constant_dynamic-update-slice_fusion.2
  445.6 1.4 collective-permute-start.9
  447.4 1.7 constant_dynamic-update-slice_fusion.5
  449.0 6.4 %collective-permute-done.4 = bf16[512,1536]{0,1:T(8,128)(2,1)} collective-permute-done((bf16[512,1536]{0,1:T(8,128)(2,1)}, bf16[512,1536]{0,1:T(8,128)(2,1)}, u32[]{:S(2)}, u32[]{:S(2)}) %collective-permute-start.4) | collective-permute-done | bytes 1572896 | tf_op jit(solution)/shard_map/ppermute | solution.py:59
  455.5 1.7 constant_dynamic-update-slice_fusion.4
  458.0 1.1 broadcast_in_dim.32
  459.1 1.9 constant_dynamic-update-slice_fusion.3
  461.0 6.5 %collective-permute-done.10 = bf16[128,2048]{1,0:T(8,128)(2,1)} collective-permute-done((bf16[128,2048]{1,0:T(8,128)(2,1)}, bf16[128,2048]{1,0:T(8,128)(2,1)}, u32[]{:S(2)}, u32[]{:S(2)}) %collective-permute-start.10) | collective-permute-done | bytes 524320 | tf_op jit(solution)/shard_map/ppermute | solution.py:59
  467.5 1.9 constant_dynamic-update-slice_fusion
  470.0 8.0 %convert_element_type.105 = f32[2048,1408]{1,0:T(8,128)} convert(bf16[2048,1408]{1,0:T(8,128)(2,1)} %get-tuple-element.53) | non-fusion elementwise | flops 2883584 | bytes 17301504 | tf_op jit(solution)/shard_map/convert_element_type | solution.py:1120
  477.9 7.9 %convert_element_type.106 = f32[2048,1408]{1,0:T(8,128)} convert(bf16[2048,1408]{1,0:T(8,128)(2,1)} %get-tuple-element.54) | non-fusion elementwise | flops 2883584 | bytes 17301504 | tf_op jit(solution)/shard_map/convert_element_type | solution.py:1120
  485.9 6.0 %convert_element_type.107 = f32[1408,2048]{1,0:T(8,128)} convert(bf16[1408,2048]{1,0:T(8,128)(2,1)S(1)} %bitcast.21) | non-fusion elementwise | flops 2883584 | bytes 17301504 | tf_op jit(solution)/shard_map/convert_element_type | solution.py:1120
  492.5 2.5 broadcast_in_dim.31
  495.0 2.8 convert_dynamic-update-slice_fusion.3
  497.8 2.8 convert_dynamic-update-slice_fusion.2
  500.6 6.1 %broadcast_in_dim.28 = f32[2048,1536]{0,1:T(8,128)} broadcast(f32[]{:T(128)} %constant.68.clone.1), dimensions={} | broadcast | bytes 12582916 | tf_op jit(solution)/shard_map/broadcast_in_dim | solution.py:87
  506.7 3.3 convert_dynamic-update-slice_fusion.1
  510.1 5.3 %convert_dynamic-update-slice_fusion = f32[2048,1536]{0,1:T(8,128)} fusion(f32[2048,1536]{0,1:T(8,128)} %convert_dynamic-update-slice_fusion.1, s32[]{:T(128)S(6)} %select_n.115, bf16[1024,1536]{0,1:T(8,128)(2,1)} %collective-permute-done.5), kind=kLoop, calls=%fused_computation | loop fusion | flops 1572864 | bytes 9437188 | tf_op jit(solution)/shard_map/dynamic_update_slice | solution.py:89
  515.4 12.7 %copy.26 = f32[2048,3,512]{2,0,1:T(8,128)} copy(f32[2048,3,512]{0,2,1:T(8,128)} %bitcast.7) | data formatting | bytes 25165824
  528.1 0.8 copy.41
  528.9 1.0 copy.42
  (42 shorter events, 3.5 us)
Async XLA Ops:
  359.3 11.4 %copy-start.1 = (bf16[512,1536]{1,0:T(8,128)(2,1)S(1)}, bf16[512,1536]{1,0:T(8,128)(2,1)}, u32[]{:S(2)}) copy-start(bf16[512,1536]{1,0:T(8,128)(2,1)} %get-tuple-element.51) | copy-start | bytes 4718596
  364.6 6.0 %collective-permute-start = (bf16[1024,1536]{1,0:T(8,128)(2,1)}, bf16[1024,1536]{1,0:T(8,128)(2,1)}, u32[]{:S(2)}, u32[]{:S(2)}) collective-permute-start(bf16[1024,1536]{1,0:T(8,128)(2,1)} %convolution_convert_fusion), channel_id=1, source_target_pairs={{0,4},{4,0},{8,12},{12,8},{16,20},{20,16},{24,28},{28,24},{1,5},{5... | collective-permute-start | bytes 9437192 | tf_op jit(solution)/shard_map/ppermute | solution.py:59
  374.4 20.7 %collective-permute-start.1 = (bf16[512,1536]{1,0:T(8,128)(2,1)}, bf16[512,1536]{1,0:T(8,128)(2,1)}, u32[]{:S(2)}, u32[]{:S(2)}) collective-permute-start(bf16[512,1536]{1,0:T(8,128)(2,1)} %add_convert_fusion), channel_id=1, source_target_pairs={{0,8},{4,20},{8,0},{12,28},{16,24},{20,4},{24,16},{28,12},{1,9},{5... | collective-permute-start | bytes 4718600 | tf_op jit(solution)/shard_map/ppermute | solution.py:59
  374.4 23.4 %copy-start = (bf16[512,2048]{1,0:T(8,128)(2,1)S(1)}, bf16[512,2048]{1,0:T(8,128)(2,1)}, u32[]{:S(2)}) copy-start(bf16[512,2048]{1,0:T(8,128)(2,1)} %get-tuple-element.52) | copy-start | bytes 6291460
  374.4 23.4 %copy-start.3 = (bf16[512,512]{1,0:T(8,128)(2,1)S(1)}, bf16[512,512]{1,0:T(8,128)(2,1)}, u32[]{:S(2)}) copy-start(bf16[512,512]{1,0:T(8,128)(2,1)} %get-tuple-element.45.refs_19_) | copy-start | bytes 1572868
  397.7 12.2 %collective-permute-start.2 = (bf16[256,1536]{1,0:T(8,128)(2,1)S(1)}, bf16[256,1536]{1,0:T(8,128)(2,1)}, u32[]{:S(2)}, u32[]{:S(2)}) collective-permute-start(bf16[256,1536]{1,0:T(8,128)(2,1)S(1)} %add_convert_fusion.2), channel_id=1, source_target_pairs={{0,16},{4,12},{8,24},{12,4},{16,0},{20,28},{24,8},{28,20},{1,17},{... | collective-permute-start | bytes 2359304 | tf_op jit(solution)/shard_map/ppermute | solution.py:59
  399.5 12.4 %collective-permute-start.6 = (bf16[256,2048]{1,0:T(8,128)(2,1)}, bf16[256,2048]{1,0:T(8,128)(2,1)}, u32[]{:S(2)}, u32[]{:S(2)}) collective-permute-start(bf16[256,2048]{1,0:T(8,128)(2,1)} %convolution_convert_fusion.1), channel_id=1, source_target_pairs={{0,4},{4,0},{8,12},{12,8},{16,20},{20,16},{24,28},{28,24},{1,5},{5... | collective-permute-start | bytes 3145736 | tf_op jit(solution)/shard_map/ppermute | solution.py:59
  411.8 17.8 %collective-permute-start.3 = (bf16[256,1536]{1,0:T(8,128)(2,1)S(1)}, bf16[256,1536]{1,0:T(8,128)(2,1)}, u32[]{:S(2)}, u32[]{:S(2)}) collective-permute-start(bf16[256,1536]{1,0:T(8,128)(2,1)S(1)} %add_convert_fusion.1), channel_id=1, source_target_pairs={{0,16},{4,12},{8,24},{12,4},{16,0},{20,28},{24,8},{28,20},{1,17},{... | collective-permute-start | bytes 2359304 | tf_op jit(solution)/shard_map/ppermute | solution.py:59
  414.3 17.7 %collective-permute-start.7 = (bf16[128,2048]{1,0:T(8,128)(2,1)}, bf16[128,2048]{1,0:T(8,128)(2,1)}, u32[]{:S(2)}, u32[]{:S(2)}) collective-permute-start(bf16[128,2048]{1,0:T(8,128)(2,1)} %add_convert_fusion.3), channel_id=1, source_target_pairs={{0,8},{4,20},{8,0},{12,28},{16,24},{20,4},{24,16},{28,12},{1,9},{5... | collective-permute-start | bytes 1572872 | tf_op jit(solution)/shard_map/ppermute | solution.py:59
  416.6 1.4 copy-start.2
  432.0 23.5 %collective-permute-start.4 = (bf16[512,1536]{0,1:T(8,128)(2,1)}, bf16[512,1536]{0,1:T(8,128)(2,1)}, u32[]{:S(2)}, u32[]{:S(2)}) collective-permute-start(bf16[512,1536]{0,1:T(8,128)(2,1)} %constant_dynamic-update-slice_fusion.6), channel_id=1, source_target_pairs={{0,8},{4,20},{8,0},{12,28},{16,24},{20,4},{24,16},{28,12},{1,9},{5... | collective-permute-start | bytes 4718600 | tf_op jit(solution)/shard_map/ppermute | solution.py:59
  433.6 9.2 %collective-permute-start.8 = (bf16[64,2048]{1,0:T(8,128)(2,1)S(1)}, bf16[64,2048]{1,0:T(8,128)(2,1)S(1)}, u32[]{:S(2)}, u32[]{:S(2)}) collective-permute-start(bf16[64,2048]{1,0:T(8,128)(2,1)S(1)} %add_convert_fusion.5), channel_id=1, source_target_pairs={{0,16},{4,12},{8,24},{12,4},{16,0},{20,28},{24,8},{28,20},{1,17},{... | collective-permute-start | bytes 786440 | tf_op jit(solution)/shard_map/ppermute | solution.py:59
  445.6 11.7 %collective-permute-start.9 = (bf16[64,2048]{1,0:T(8,128)(2,1)S(1)}, bf16[64,2048]{1,0:T(8,128)(2,1)S(1)}, u32[]{:S(2)}, u32[]{:S(2)}) collective-permute-start(bf16[64,2048]{1,0:T(8,128)(2,1)S(1)} %get-tuple-element.69), channel_id=1, source_target_pairs={{0,16},{4,12},{8,24},{12,4},{16,0},{20,28},{24,8},{28,20},{1,17},{... | collective-permute-start | bytes 786440 | tf_op jit(solution)/shard_map/ppermute | solution.py:59
  457.2 12.2 %copy-start.6 = (f32[8,2048]{1,0:T(8,128)S(1)}, f32[8,2048]{1,0:T(8,128)}, u32[]{:S(2)}) copy-start(f32[8,2048]{1,0:T(8,128)} %get-tuple-element.49) | copy-start | bytes 196612
  457.2 52.9 %collective-permute-start.5 = (bf16[1024,1536]{0,1:T(8,128)(2,1)S(1)}, bf16[1024,1536]{0,1:T(8,128)(2,1)}, u32[]{:S(2)}, u32[]{:S(2)}) collective-permute-start(bf16[1024,1536]{0,1:T(8,128)(2,1)S(1)} %constant_dynamic-update-slice_fusion.4), channel_id=1, source_target_pairs={{0,4},{4,0},{8,12},{12,8},{16,20},{20,16},{24,28},{28,24},{1,5},{5... | collective-permute-start | bytes 9437192 | tf_op jit(solution)/shard_map/ppermute | solution.py:59
  458.0 9.5 %collective-permute-start.10 = (bf16[128,2048]{1,0:T(8,128)(2,1)}, bf16[128,2048]{1,0:T(8,128)(2,1)}, u32[]{:S(2)}, u32[]{:S(2)}) collective-permute-start(bf16[128,2048]{1,0:T(8,128)(2,1)} %constant_dynamic-update-slice_fusion.1), channel_id=1, source_target_pairs={{0,8},{4,20},{8,0},{12,28},{16,24},{20,4},{24,16},{28,12},{1,9},{5... | collective-permute-start | bytes 1572872 | tf_op jit(solution)/shard_map/ppermute | solution.py:59
  469.4 28.4 %collective-permute-start.11 = (bf16[256,2048]{1,0:T(8,128)(2,1)}, bf16[256,2048]{1,0:T(8,128)(2,1)}, u32[]{:S(2)}, u32[]{:S(2)}) collective-permute-start(bf16[256,2048]{1,0:T(8,128)(2,1)} %constant_dynamic-update-slice_fusion), channel_id=1, source_target_pairs={{0,4},{4,0},{8,12},{12,8},{16,20},{20,16},{24,28},{28,24},{1,5},{5... | collective-permute-start | bytes 3145736 | tf_op jit(solution)/shard_map/ppermute | solution.py:59
  470.0 15.9 %slice-start = ((s8[5767168]{0:T(1024)(128)(4,1)}), s8[4194304]{0:T(1024)(128)(4,1)S(1)}, s32[]{:S(2)}) async-start(s8[5767168]{0:T(1024)(128)(4,1)} %bitcast.20), calls=%async_computation | async-start | bytes 8388608
  477.9 7.9 %slice-start.1 = ((s8[5767168]{0:T(1024)(128)(4,1)}), s8[1572864]{0:T(1024)(128)(4,1)S(1)}, s32[]{:S(2)}) async-start(s8[5767168]{0:T(1024)(128)(4,1)} %bitcast.20), calls=%async_computation.1 | async-start | bytes 3145728
  515.4 12.7 %copy-start.5 = (bf16[128,2048]{1,0:T(8,128)(2,1)S(1)}, bf16[128,2048]{1,0:T(8,128)(2,1)}, u32[]{:S(2)}) copy-start(bf16[128,2048]{1,0:T(8,128)(2,1)} %get-tuple-element.89) | copy-start | bytes 1572868
  515.4 13.5 %copy-start.4 = (f32[128,2048]{1,0:T(8,128)S(1)}, f32[128,2048]{1,0:T(8,128)}, u32[]{:S(2)}) copy-start(f32[128,2048]{1,0:T(8,128)} %get-tuple-element.90) | copy-start | bytes 3145732
